TPU v7x, 1024 devices: a whole 8x8x8 slice. The times are simulated.
1024 devices in a mesh: gx: 32 (over x, z_hi, core), gy: 32 (over y, z_lo).
Axes of the slice: x: 8, y: 8, z: 8 (z_hi: 2, z_lo: 4; z = z_hi * 4 + z_lo), core: 2. Of those that a mesh axis runs over, the one named last changes fastest.
Arguments:
- populations: float32 [19, 512, 16384], P(None, 'gx', 'gy'), may hold values from 0.5 to 1.5
- tracer: float32 [7, 512, 16384], P(None, 'gx', 'gy'), may hold values from 0.2 to 2
- solid_mask: int32 [512, 16384], P('gx', 'gy'), may hold values 0 or 1
- inflow: int32 [512, 16384], P('gx', 'gy'), may hold values 0 or 1
- wind_profile: float32 [3, 32], replicated, may hold values from -0.12 to 0.12
- emission: float32 [512, 16384], P('gx', 'gy'), may hold values from 0.05 to 0.5
Outputs:
- final_populations: float32 [19, 512, 16384], P(None, 'gx', 'gy')
- final_tracer: float32 [7, 512, 16384], P(None, 'gx', 'gy')
All inputs are finite; a program needn't handle non-finite values. No bound on the sum of `solid_mask` or of `inflow` on one device may be relied on, other than what follows from the above.
Results may differ from a plain program's by a relative error of at most 0.0001.
Values sent between devices are 32-bit elements; how exact they have to be, the bound alone decides.
A program may use at most 32 MiB of HBM per device.

v0:
```python
import math

import jax
import jax.numpy as jnp
from jax import lax
from jax.sharding import PartitionSpec as P

NZ = 32
STEPS = 4


LATTICE = (
    (0, 0, 0),
    (1, 0, 0),
    (-1, 0, 0),
    (0, 1, 0),
    (0, -1, 0),
    (0, 0, 1),
    (0, 0, -1),
    (1, 1, 0),
    (-1, -1, 0),
    (1, -1, 0),
    (-1, 1, 0),
    (1, 0, 1),
    (-1, 0, -1),
    (1, 0, -1),
    (-1, 0, 1),
    (0, 1, 1),
    (0, -1, -1),
    (0, 1, -1),
    (0, -1, 1),
)
OPPOSITE = (0, 2, 1, 4, 3, 6, 5, 8, 7, 10, 9, 12, 11, 14, 13, 16, 15, 18, 17)
WEIGHTS = (1.0 / 3.0,) + (1.0 / 18.0,) * 6 + (1.0 / 36.0,) * 12
TRACER_LATTICE = LATTICE[:7]
TRACER_OPPOSITE = OPPOSITE[:7]
TRACER_WEIGHTS = (0.25,) + (0.125,) * 6
BASE_RELAX = 0.6
SMAGORINSKY = 0.2
TRACER_RELAX = 0.7


def passed_along(shard, axis, by):
    length = lax.axis_size(axis)
    return lax.ppermute(shard, axis, [(i, (i + by) % length) for i in range(length)])


def projection(index, speed, lattice):
    return sum(
        (lattice[index][axis] * speed[axis] for axis in range(3) if lattice[index][axis] != 0)
    )


def equilibrium(rate, speed, speed_sq, index):
    along = projection(index, speed, LATTICE)
    return rate + 3.0 * along + 4.5 * along * along - 1.5 * speed_sq


def collide(populations, tracer, solid_mask, inflow, wind_profile, emission):
    width = populations.shape[2]
    wind_cells = jnp.tile(wind_profile, (1, width // wind_profile.shape[1]))[:, None, :]
    normal = [populations[k] for k in range(19)]
    density = sum((WEIGHTS[k] * normal[k] for k in range(19)))
    velocity = [
        sum((WEIGHTS[k] * LATTICE[k][axis] * normal[k] for k in range(19) if LATTICE[k][axis] != 0))
        for axis in range(3)
    ]
    speed_sq = velocity[0] * velocity[0] + velocity[1] * velocity[1] + velocity[2] * velocity[2]
    deviation = [normal[k] - equilibrium(density, velocity, speed_sq, k) for k in range(19)]
    contraction = 0.0
    for first in range(3):
        for second in range(first, 3):
            stress = sum(
                (
                    WEIGHTS[k] * LATTICE[k][first] * LATTICE[k][second] * deviation[k]
                    for k in range(19)
                    if LATTICE[k][first] * LATTICE[k][second] != 0
                )
            )
            factor = 1.0 if first == second else 2.0
            contraction = contraction + factor * stress * stress
    relax_time = 0.5 * (
        BASE_RELAX
        + jnp.sqrt(
            BASE_RELAX * BASE_RELAX
            + 18.0 * math.sqrt(2.0) * SMAGORINSKY * SMAGORINSKY * jnp.sqrt(contraction)
        )
    )
    wind_sq = (
        wind_cells[0] * wind_cells[0]
        + wind_cells[1] * wind_cells[1]
        + wind_cells[2] * wind_cells[2]
    )
    is_solid = solid_mask == 1
    is_inflow = inflow == 1
    relaxed = []
    for k in range(19):
        held = equilibrium(1.0, wind_cells, wind_sq, k)
        fluid = normal[k] - deviation[k] / relax_time
        relaxed.append(jnp.where(is_solid, normal[OPPOSITE[k]], jnp.where(is_inflow, held, fluid)))
    amount = [tracer[k] for k in range(7)]
    concentration = sum((TRACER_WEIGHTS[k] * amount[k] for k in range(7)))
    traced = []
    for k in range(7):
        balance = concentration * (1.0 + 4.0 * projection(k, velocity, TRACER_LATTICE))
        updated = amount[k] - (amount[k] - balance) / TRACER_RELAX + emission
        traced.append(
            jnp.where(is_solid, amount[TRACER_OPPOSITE[k]], jnp.where(is_inflow, 0.0, updated))
        )
    return (jnp.stack(relaxed), jnp.stack(traced))


def margin_east_west(pieces, offset):
    first, second, third = pieces
    return passed_along((first, second, third), "gx", offset)


def margin_north_south(pieces, offset):
    first, second, third = pieces
    return passed_along((first, second, third), "gy", offset)


def local_stream(relaxed, lattice, opposite):
    number, extent_x, width = relaxed.shape
    padded = jnp.pad(relaxed, ((0, 0), (1, 1), (NZ + 1, NZ + 1)))
    height = lax.iota(jnp.int32, width) % NZ
    layers = []
    for k in range(number):
        step_x, step_y, step_z = lattice[k]
        offset = 1 + NZ - step_y * NZ - step_z
        shifted = padded[k, 1 - step_x : 1 - step_x + extent_x, offset : offset + width]
        if step_z == 1:
            shifted = jnp.where(height >= 1, shifted, relaxed[opposite[k]])
        elif step_z == -1:
            shifted = jnp.where(height <= NZ - 2, shifted, relaxed[opposite[k]])
        layers.append(shifted)
    return jnp.stack(layers)


def margin_run(populations, tracer, solid_mask, inflow, wind_profile, emission):
    depth = STEPS
    block_x = populations.shape[1]
    width = populations.shape[2]
    fields = jnp.stack([solid_mask.astype(jnp.float32), inflow.astype(jnp.float32), emission])
    pieces = (populations, tracer, fields)
    west_part = margin_east_west(tuple((p[:, block_x - depth :] for p in pieces)), 1)
    east_part = margin_east_west(tuple((p[:, :depth] for p in pieces)), -1)
    wide = tuple((jnp.concatenate([w, p, e], 1) for w, p, e in zip(west_part, pieces, east_part)))
    south_part = margin_north_south(tuple((p[:, :, width - depth * NZ :] for p in wide)), 1)
    north_part = margin_north_south(tuple((p[:, :, : depth * NZ] for p in wide)), -1)
    grown = tuple((jnp.concatenate([s, p, n], 2) for s, p, n in zip(south_part, wide, north_part)))
    flow, amount, cell_fields = grown
    solid_grown = jnp.where(cell_fields[0] == 1.0, 1, 0).astype(jnp.int32)
    inflow_grown = jnp.where(cell_fields[1] == 1.0, 1, 0).astype(jnp.int32)
    for iteration in range(STEPS):
        relaxed, traced = collide(
            flow, amount, solid_grown, inflow_grown, wind_profile, cell_fields[2]
        )
        flow = local_stream(relaxed, LATTICE, OPPOSITE)
        amount = local_stream(traced, TRACER_LATTICE, TRACER_OPPOSITE)
    low = depth * NZ
    return (
        flow[:, depth : depth + block_x, low : low + width],
        amount[:, depth : depth + block_x, low : low + width],
    )


def local(populations, tracer, solid_mask, inflow, wind_profile, emission):
    return margin_run(populations, tracer, solid_mask, inflow, wind_profile, emission)


def solution(mesh):
    in_specs = (
        P(None, "gx", "gy"),
        P(None, "gx", "gy"),
        P("gx", "gy"),
        P("gx", "gy"),
        P(),
        P("gx", "gy"),
    )
    out_specs = (P(None, "gx", "gy"), P(None, "gx", "gy"))
    return jax.shard_map(local, mesh=mesh, in_specs=in_specs, out_specs=out_specs, check_vma=False)
```

profile of v0, /device:TPU:8, one launch (start us, length us, event | category | flops | bytes accessed | tf_op | source)
XLA Modules:
  0.0 107.8 jit_solution(813088672122424535)
XLA Ops:
  0.7 0.8 convert_bitcast_fusion
  2.2 1.9 %collective-permute-start = (f32[3,4,512]{2,1,0:T(4,128)S(1)}, f32[3,4,512]{2,1,0:T(4,128)S(1)}, u32[]{:S(2)}, u32[]{:S(2)}) collective-permute-start(f32[3,4,512]{2,1,0:T(4,128)S(1)} %get-tuple-element.244), channel_id=1, source_target_pairs={{0,32},{32,64},{64,96},{96,128},{128,160},{160,192},{192,224},{224... | collective-permute-start | bytes 73736 | tf_op jit(solution)/shard_map/ppermute | solution.py:45
  4.2 14.0 %collective-permute-start.1 = (f32[3,4,512]{2,1,0:T(4,128)S(1)}, f32[3,4,512]{2,1,0:T(4,128)S(1)}, u32[]{:S(2)}, u32[]{:S(2)}) collective-permute-start(f32[3,4,512]{2,1,0:T(4,128)S(1)} %get-tuple-element.245), channel_id=1, source_target_pairs={{0,992},{32,0},{64,32},{96,64},{128,96},{160,128},{192,160},{224,1... | collective-permute-start | bytes 73736 | tf_op jit(solution)/shard_map/ppermute | solution.py:45
  18.1 1.0 fusion.483
  19.1 2.6 %collective-permute-start.8 = (f32[7,4,512]{2,1,0:T(4,128)S(1)}, f32[7,4,512]{2,1,0:T(4,128)S(1)}, u32[]{:S(2)}, u32[]{:S(2)}) collective-permute-start(f32[7,4,512]{2,1,0:T(4,128)S(1)} %get-tuple-element.234), channel_id=1, source_target_pairs={{0,32},{32,64},{64,96},{96,128},{128,160},{160,192},{192,224},{224... | collective-permute-start | bytes 172040 | tf_op jit(solution)/shard_map/ppermute | solution.py:45
  21.7 9.1 %collective-permute-start.9 = (f32[7,4,512]{2,1,0:T(4,128)S(1)}, f32[7,4,512]{2,1,0:T(4,128)S(1)}, u32[]{:S(2)}, u32[]{:S(2)}) collective-permute-start(f32[7,4,512]{2,1,0:T(4,128)S(1)} %get-tuple-element.235), channel_id=1, source_target_pairs={{0,992},{32,0},{64,32},{96,64},{128,96},{160,128},{192,160},{224,1... | collective-permute-start | bytes 172040 | tf_op jit(solution)/shard_map/ppermute | solution.py:45
  30.8 1.1 %fusion.482 = (f32[19,4,512]{2,1,0:T(4,128)S(1)}, f32[19,4,512]{2,1,0:T(4,128)S(1)}) fusion(f32[19,16,512]{2,1,0:T(8,128)} %param.6), kind=kLoop, calls=%fused_computation.853 | loop fusion | bytes 622592 | tf_op jit(solution)/shard_map/slice | solution.py:146
  32.0 1.9 %collective-permute-start.4 = (f32[19,4,512]{2,1,0:T(4,128)S(1)}, f32[19,4,512]{2,1,0:T(4,128)S(1)}, u32[]{:S(2)}, u32[]{:S(2)}) collective-permute-start(f32[19,4,512]{2,1,0:T(4,128)S(1)} %get-tuple-element.230), channel_id=1, source_target_pairs={{0,32},{32,64},{64,96},{96,128},{128,160},{160,192},{192,224},{224... | collective-permute-start | bytes 466952 | tf_op jit(solution)/shard_map/ppermute | solution.py:45
  33.9 0.8 slice_bitcast_fusion.2
  35.0 9.7 %collective-permute-start.5 = (f32[19,4,512]{2,1,0:T(4,128)S(1)}, f32[19,4,512]{2,1,0:T(4,128)S(1)}, u32[]{:S(2)}, u32[]{:S(2)}) collective-permute-start(f32[19,4,512]{2,1,0:T(4,128)S(1)} %get-tuple-element.231), channel_id=1, source_target_pairs={{0,992},{32,0},{64,32},{96,64},{128,96},{160,128},{192,160},{224,1... | collective-permute-start | bytes 466952 | tf_op jit(solution)/shard_map/ppermute | solution.py:45
  45.4 4.3 %collective-permute-start.2 = (f32[3,24,128]{2,1,0:T(8,128)S(1)}, f32[3,24,128]{2,1,0:T(8,128)S(1)}, u32[]{:S(2)}, u32[]{:S(2)}) collective-permute-start(f32[3,24,128]{2,1,0:T(8,128)S(1)} %get-tuple-element.236), channel_id=1, source_target_pairs={{0,1},{1,2},{2,3},{3,4},{4,5},{5,6},{6,7},{7,8},{8,9},{9,10},{10,1... | collective-permute-start | bytes 110600 | tf_op jit(solution)/shard_map/ppermute | solution.py:45
  49.7 9.3 %collective-permute-start.3 = (f32[3,24,128]{2,1,0:T(8,128)S(1)}, f32[3,24,128]{2,1,0:T(8,128)S(1)}, u32[]{:S(2)}, u32[]{:S(2)}) collective-permute-start(f32[3,24,128]{2,1,0:T(8,128)S(1)} %get-tuple-element.237), channel_id=1, source_target_pairs={{0,31},{1,0},{2,1},{3,2},{4,3},{5,4},{6,5},{7,6},{8,7},{9,8},{10,9... | collective-permute-start | bytes 110600 | tf_op jit(solution)/shard_map/ppermute | solution.py:45
  59.0 1.9 %collective-permute-start.10 = (f32[7,24,128]{2,1,0:T(8,128)S(1)}, f32[7,24,128]{2,1,0:T(8,128)S(1)}, u32[]{:S(2)}, u32[]{:S(2)}) collective-permute-start(f32[7,24,128]{2,1,0:T(8,128)S(1)} %get-tuple-element.232), channel_id=1, source_target_pairs={{0,1},{1,2},{2,3},{3,4},{4,5},{5,6},{6,7},{7,8},{8,9},{9,10},{10,1... | collective-permute-start | bytes 258056 | tf_op jit(solution)/shard_map/ppermute | solution.py:45
  61.0 7.8 %collective-permute-start.11 = (f32[7,24,128]{2,1,0:T(8,128)S(1)}, f32[7,24,128]{2,1,0:T(8,128)S(1)}, u32[]{:S(2)}, u32[]{:S(2)}) collective-permute-start(f32[7,24,128]{2,1,0:T(8,128)S(1)} %get-tuple-element.233), channel_id=1, source_target_pairs={{0,31},{1,0},{2,1},{3,2},{4,3},{5,4},{6,5},{7,6},{8,7},{9,8},{10,9... | collective-permute-start | bytes 258056 | tf_op jit(solution)/shard_map/ppermute | solution.py:45
  69.3 1.6 %collective-permute-done.11 = f32[7,24,128]{2,1,0:T(8,128)S(1)} collective-permute-done((f32[7,24,128]{2,1,0:T(8,128)S(1)}, f32[7,24,128]{2,1,0:T(8,128)S(1)}, u32[]{:S(2)}, u32[]{:S(2)}) %collective-permute-start.11) | collective-permute-done | bytes 86048 | tf_op jit(solution)/shard_map/ppermute | solution.py:45
  71.1 1.9 %collective-permute-start.6 = (f32[19,24,128]{2,1,0:T(8,128)S(1)}, f32[19,24,128]{2,1,0:T(8,128)S(1)}, u32[]{:S(2)}, u32[]{:S(2)}) collective-permute-start(f32[19,24,128]{2,1,0:T(8,128)S(1)} %get-tuple-element.228), channel_id=1, source_target_pairs={{0,1},{1,2},{2,3},{3,4},{4,5},{5,6},{6,7},{7,8},{8,9},{9,10},{10,1... | collective-permute-start | bytes 700424 | tf_op jit(solution)/shard_map/ppermute | solution.py:45
  73.0 8.3 %collective-permute-start.7 = (f32[19,24,128]{2,1,0:T(8,128)S(1)}, f32[19,24,128]{2,1,0:T(8,128)S(1)}, u32[]{:S(2)}, u32[]{:S(2)}) collective-permute-start(f32[19,24,128]{2,1,0:T(8,128)S(1)} %get-tuple-element.229), channel_id=1, source_target_pairs={{0,31},{1,0},{2,1},{3,2},{4,3},{5,4},{6,5},{7,6},{8,7},{9,8},{10,9... | collective-permute-start | bytes 700424 | tf_op jit(solution)/shard_map/ppermute | solution.py:45
  81.4 2.1 %collective-permute-done.6 = f32[19,24,128]{2,1,0:T(8,128)S(1)} collective-permute-done((f32[19,24,128]{2,1,0:T(8,128)S(1)}, f32[19,24,128]{2,1,0:T(8,128)S(1)}, u32[]{:S(2)}, u32[]{:S(2)}) %collective-permute-start.6) | collective-permute-done | bytes 233504 | tf_op jit(solution)/shard_map/ppermute | solution.py:45
  83.5 1.4 %collective-permute-done.7 = f32[19,24,128]{2,1,0:T(8,128)S(1)} collective-permute-done((f32[19,24,128]{2,1,0:T(8,128)S(1)}, f32[19,24,128]{2,1,0:T(8,128)S(1)}, u32[]{:S(2)}, u32[]{:S(2)}) %collective-permute-start.7) | collective-permute-done | bytes 233504 | tf_op jit(solution)/shard_map/ppermute | solution.py:45
  85.5 0.7 constant_dynamic-update-slice_fusion.18
  86.7 1.0 constant_dynamic-update-slice_fusion.7
  87.6 1.0 constant_dynamic-update-slice_fusion.6
  88.6 1.0 constant_dynamic-update-slice_fusion.5
  89.5 1.0 constant_dynamic-update-slice_fusion.4
  90.5 1.0 constant_dynamic-update-slice_fusion.3
  91.5 1.0 constant_dynamic-update-slice_fusion.2
  92.4 1.0 constant_dynamic-update-slice_fusion.1
  93.4 1.1 %constant_dynamic-update-slice_fusion = (f32[19,24,768]{2,1,0:T(8,128)S(1)}, f32[1,24,768]{2,1,0:T(8,128)S(1)}, f32[7,24,768]{2,1,0:T(8,128)S(1)}, f32[1,24,768]...) fusion(f32[19,24,768]{2,1,0:T(8,128)S(1)} %get-tuple-element.189, ...), kind=kLoop, calls=%fused_computation.98 | loop fusion | flops 460799 | bytes 1665024 | tf_op jit(solution)/shard_map/stack | solution.py:110
  95.4 0.9 constant_dynamic-update-slice_fusion.37
  98.7 0.9 constant_dynamic-update-slice_fusion.56
  102.0 1.0 select_select_fusion.22
  106.9 0.9 slice.765
  (146 shorter events, 12.6 us)
Async XLA Ops:
  0.6 68.2 %copy-start.3 = (f32[16,512]{1,0:T(8,128)S(1)}, f32[16,512]{1,0:T(8,128)}, u32[]{:S(2)}) copy-start(f32[16,512]{1,0:T(8,128)} %param.11) | copy-start | bytes 98308
  0.6 58.4 %copy-start.2 = (f32[7,16,512]{2,1,0:T(8,128)S(1)}, f32[7,16,512]{2,1,0:T(8,128)}, u32[]{:S(2)}) copy-start(f32[7,16,512]{2,1,0:T(8,128)} %param.7) | copy-start | bytes 688132
  2.2 32.8 %collective-permute-start = (f32[3,4,512]{2,1,0:T(4,128)S(1)}, f32[3,4,512]{2,1,0:T(4,128)S(1)}, u32[]{:S(2)}, u32[]{:S(2)}) collective-permute-start(f32[3,4,512]{2,1,0:T(4,128)S(1)} %get-tuple-element.244), channel_id=1, source_target_pairs={{0,32},{32,64},{64,96},{96,128},{128,160},{160,192},{192,224},{224... | collective-permute-start | bytes 73736 | tf_op jit(solution)/shard_map/ppermute | solution.py:45
  4.2 40.5 %collective-permute-start.1 = (f32[3,4,512]{2,1,0:T(4,128)S(1)}, f32[3,4,512]{2,1,0:T(4,128)S(1)}, u32[]{:S(2)}, u32[]{:S(2)}) collective-permute-start(f32[3,4,512]{2,1,0:T(4,128)S(1)} %get-tuple-element.245), channel_id=1, source_target_pairs={{0,992},{32,0},{64,32},{96,64},{128,96},{160,128},{192,160},{224,1... | collective-permute-start | bytes 73736 | tf_op jit(solution)/shard_map/ppermute | solution.py:45
  19.1 30.6 %collective-permute-start.8 = (f32[7,4,512]{2,1,0:T(4,128)S(1)}, f32[7,4,512]{2,1,0:T(4,128)S(1)}, u32[]{:S(2)}, u32[]{:S(2)}) collective-permute-start(f32[7,4,512]{2,1,0:T(4,128)S(1)} %get-tuple-element.234), channel_id=1, source_target_pairs={{0,32},{32,64},{64,96},{96,128},{128,160},{160,192},{192,224},{224... | collective-permute-start | bytes 172040 | tf_op jit(solution)/shard_map/ppermute | solution.py:45
  21.7 49.3 %copy-start.1 = (f32[19,16,512]{2,1,0:T(8,128)S(1)}, f32[19,16,512]{2,1,0:T(8,128)}, u32[]{:S(2)}) copy-start(f32[19,16,512]{2,1,0:T(8,128)} %param.6) | copy-start | bytes 1867780
  21.7 37.3 %collective-permute-start.9 = (f32[7,4,512]{2,1,0:T(4,128)S(1)}, f32[7,4,512]{2,1,0:T(4,128)S(1)}, u32[]{:S(2)}, u32[]{:S(2)}) collective-permute-start(f32[7,4,512]{2,1,0:T(4,128)S(1)} %get-tuple-element.235), channel_id=1, source_target_pairs={{0,992},{32,0},{64,32},{96,64},{128,96},{160,128},{192,160},{224,1... | collective-permute-start | bytes 172040 | tf_op jit(solution)/shard_map/ppermute | solution.py:45
  32.0 39.0 %collective-permute-start.4 = (f32[19,4,512]{2,1,0:T(4,128)S(1)}, f32[19,4,512]{2,1,0:T(4,128)S(1)}, u32[]{:S(2)}, u32[]{:S(2)}) collective-permute-start(f32[19,4,512]{2,1,0:T(4,128)S(1)} %get-tuple-element.230), channel_id=1, source_target_pairs={{0,32},{32,64},{64,96},{96,128},{128,160},{160,192},{192,224},{224... | collective-permute-start | bytes 466952 | tf_op jit(solution)/shard_map/ppermute | solution.py:45
  35.0 36.0 %collective-permute-start.5 = (f32[19,4,512]{2,1,0:T(4,128)S(1)}, f32[19,4,512]{2,1,0:T(4,128)S(1)}, u32[]{:S(2)}, u32[]{:S(2)}) collective-permute-start(f32[19,4,512]{2,1,0:T(4,128)S(1)} %get-tuple-element.231), channel_id=1, source_target_pairs={{0,992},{32,0},{64,32},{96,64},{128,96},{160,128},{192,160},{224,1... | collective-permute-start | bytes 466952 | tf_op jit(solution)/shard_map/ppermute | solution.py:45
  45.4 15.6 %collective-permute-start.2 = (f32[3,24,128]{2,1,0:T(8,128)S(1)}, f32[3,24,128]{2,1,0:T(8,128)S(1)}, u32[]{:S(2)}, u32[]{:S(2)}) collective-permute-start(f32[3,24,128]{2,1,0:T(8,128)S(1)} %get-tuple-element.236), channel_id=1, source_target_pairs={{0,1},{1,2},{2,3},{3,4},{4,5},{5,6},{6,7},{7,8},{8,9},{9,10},{10,1... | collective-permute-start | bytes 110600 | tf_op jit(solution)/shard_map/ppermute | solution.py:45
  49.7 19.1 %collective-permute-start.3 = (f32[3,24,128]{2,1,0:T(8,128)S(1)}, f32[3,24,128]{2,1,0:T(8,128)S(1)}, u32[]{:S(2)}, u32[]{:S(2)}) collective-permute-start(f32[3,24,128]{2,1,0:T(8,128)S(1)} %get-tuple-element.237), channel_id=1, source_target_pairs={{0,31},{1,0},{2,1},{3,2},{4,3},{5,4},{6,5},{7,6},{8,7},{9,8},{10,9... | collective-permute-start | bytes 110600 | tf_op jit(solution)/shard_map/ppermute | solution.py:45
  59.0 10.3 %collective-permute-start.10 = (f32[7,24,128]{2,1,0:T(8,128)S(1)}, f32[7,24,128]{2,1,0:T(8,128)S(1)}, u32[]{:S(2)}, u32[]{:S(2)}) collective-permute-start(f32[7,24,128]{2,1,0:T(8,128)S(1)} %get-tuple-element.232), channel_id=1, source_target_pairs={{0,1},{1,2},{2,3},{3,4},{4,5},{5,6},{6,7},{7,8},{8,9},{9,10},{10,1... | collective-permute-start | bytes 258056 | tf_op jit(solution)/shard_map/ppermute | solution.py:45
  61.0 9.9 %collective-permute-start.11 = (f32[7,24,128]{2,1,0:T(8,128)S(1)}, f32[7,24,128]{2,1,0:T(8,128)S(1)}, u32[]{:S(2)}, u32[]{:S(2)}) collective-permute-start(f32[7,24,128]{2,1,0:T(8,128)S(1)} %get-tuple-element.233), channel_id=1, source_target_pairs={{0,31},{1,0},{2,1},{3,2},{4,3},{5,4},{6,5},{7,6},{8,7},{9,8},{10,9... | collective-permute-start | bytes 258056 | tf_op jit(solution)/shard_map/ppermute | solution.py:45
  71.1 12.4 %collective-permute-start.6 = (f32[19,24,128]{2,1,0:T(8,128)S(1)}, f32[19,24,128]{2,1,0:T(8,128)S(1)}, u32[]{:S(2)}, u32[]{:S(2)}) collective-permute-start(f32[19,24,128]{2,1,0:T(8,128)S(1)} %get-tuple-element.228), channel_id=1, source_target_pairs={{0,1},{1,2},{2,3},{3,4},{4,5},{5,6},{6,7},{7,8},{8,9},{9,10},{10,1... | collective-permute-start | bytes 700424 | tf_op jit(solution)/shard_map/ppermute | solution.py:45
  73.0 11.8 %collective-permute-start.7 = (f32[19,24,128]{2,1,0:T(8,128)S(1)}, f32[19,24,128]{2,1,0:T(8,128)S(1)}, u32[]{:S(2)}, u32[]{:S(2)}) collective-permute-start(f32[19,24,128]{2,1,0:T(8,128)S(1)} %get-tuple-element.229), channel_id=1, source_target_pairs={{0,31},{1,0},{2,1},{3,2},{4,3},{5,4},{6,5},{7,6},{8,7},{9,8},{10,9... | collective-permute-start | bytes 700424 | tf_op jit(solution)/shard_map/ppermute | solution.py:45
  85.0 1.6 %copy-start = (f32[19,24,768]{2,1,0:T(8,128)}, f32[19,24,768]{2,1,0:T(8,128)S(1)}, u32[]{:S(2)}) copy-start(f32[19,24,768]{2,1,0:T(8,128)S(1)} %pad_maximum_fusion) | copy-start | bytes 4202500
where the time goes:
time: 109 us; the launch traced here: 108 us
  starting transfers between devices  72.7 us (67%)
  other arithmetic  22.5 us (21%)
  local copies, waits for them, and re-layouts  5.63 us (5%)
  waiting for transfers between devices  5.51 us (5%)
  between operations  1.5 us (1%)
    ppermute x12, starting transfers between devices, passed_along(): lax.ppermute(shard, axis, [(i, (i + by) % length) for i in range(length)])  72.7 us
    unnamed x99, other arithmetic  17 us
    ppermute x12, waiting for transfers between devices, passed_along(): lax.ppermute(shard, axis, [(i, (i + by) % length) for i in range(length)])  5.51 us
  transfers between devices with their start and end apart: 12, of which 4 were waited for; matrix products, arithmetic and copies ran while one was open for 4% of the time, Pallas kernels for 0%

commit v1 on v0

v1 whole, which is shorter than its diff:
```python
import functools
import math

import jax
import jax.numpy as jnp
from jax import lax
from jax.experimental import pallas as pl
from jax.experimental.pallas import tpu as pltpu
from jax.sharding import PartitionSpec as P

NZ = 32
STEPS = 4
FLOW = 19
TRACE = 7
POPS = FLOW + TRACE

LATTICE = (
    (0, 0, 0),
    (1, 0, 0),
    (-1, 0, 0),
    (0, 1, 0),
    (0, -1, 0),
    (0, 0, 1),
    (0, 0, -1),
    (1, 1, 0),
    (-1, -1, 0),
    (1, -1, 0),
    (-1, 1, 0),
    (1, 0, 1),
    (-1, 0, -1),
    (1, 0, -1),
    (-1, 0, 1),
    (0, 1, 1),
    (0, -1, -1),
    (0, 1, -1),
    (0, -1, 1),
)
OPPOSITE = (0, 2, 1, 4, 3, 6, 5, 8, 7, 10, 9, 12, 11, 14, 13, 16, 15, 18, 17)
MOVES = LATTICE + LATTICE[:TRACE]
BACK = OPPOSITE + tuple(FLOW + k for k in OPPOSITE[:TRACE])
BASE_RELAX = 0.6
SMAGORINSKY = 0.2
TRACER_RELAX = 0.7

SIDES = tuple(
    tuple(k for k in range(POPS) if MOVES[k][axis] == sign)
    for axis in (0, 1)
    for sign in (1, -1)
)
NEIGHBOURS = ((1, 0), (-1, 0), (0, 1), (0, -1), (1, 1), (-1, -1), (1, -1), (-1, 1))
CORNERS = (7, 8, 9, 10)
MESH = pl.DeviceIdType.MESH


def inflow_states(wind):
    square = wind[0] * wind[0] + wind[1] * wind[1] + wind[2] * wind[2]
    held = []
    for k in range(FLOW):
        along = sum(LATTICE[k][a] * wind[a] for a in range(3) if LATTICE[k][a] != 0)
        held.append(1.0 + 3.0 * along + 4.5 * along * along - 1.5 * square)
    return held


def relax_cells(h, q, solid, inflow, emission, held):
    total = {k: h[k] + h[k + 1] for k in range(1, FLOW, 2)}
    delta = {k: h[k] - h[k + 1] for k in range(1, FLOW, 2)}
    in_xy, in_xz, in_yz = total[7] + total[9], total[11] + total[13], total[15] + total[17]
    along_x, along_y, along_z = 2.0 * total[1], 2.0 * total[3], 2.0 * total[5]
    density = (
        12.0 * h[0] + ((along_x + along_y) + along_z) + ((in_xy + in_xz) + in_yz)
    ) * (1.0 / 36.0)
    speed = [
        (2.0 * delta[1] + (delta[7] + delta[9]) + (delta[11] + delta[13])) * (1.0 / 12.0),
        (2.0 * delta[3] + (delta[7] - delta[9]) + (delta[15] + delta[17])) * (1.0 / 12.0),
        (2.0 * delta[5] + (delta[11] - delta[13]) + (delta[15] - delta[17])) * (1.0 / 12.0),
    ]
    square = [v * v for v in speed]
    third = 3.0 * density
    stress_x = 0.25 * (along_x + in_xy + in_xz) - third - square[0]
    stress_y = 0.25 * (along_y + in_xy + in_yz) - third - square[1]
    stress_z = 0.25 * (along_z + in_xz + in_yz) - third - square[2]
    stress_xy = 0.25 * (total[7] - total[9]) - speed[0] * speed[1]
    stress_xz = 0.25 * (total[11] - total[13]) - speed[0] * speed[2]
    stress_yz = 0.25 * (total[15] - total[17]) - speed[1] * speed[2]
    contraction = (
        stress_x * stress_x
        + stress_y * stress_y
        + stress_z * stress_z
        + 2.0 * (stress_xy * stress_xy + stress_xz * stress_xz + stress_yz * stress_yz)
    )
    gain = 18.0 * math.sqrt(2.0) * SMAGORINSKY * SMAGORINSKY / 9.0
    rate = 2.0 / (
        BASE_RELAX + jnp.sqrt(BASE_RELAX * BASE_RELAX + gain * jnp.sqrt(contraction))
    )
    keep = 1.0 - rate
    base = rate * (density - (square[0] + square[1] + square[2]) * (1.0 / 6.0))
    half = 0.5 * rate

    def settle(k, fluid):
        return jnp.where(solid, h[OPPOSITE[k]], jnp.where(inflow, held(k), fluid))

    relaxed = [settle(0, keep * h[0] + base)]
    for k in range(1, FLOW, 2):
        along = sum(LATTICE[k][a] * speed[a] for a in range(3) if LATTICE[k][a] != 0)
        even = base + half * along * along
        odd = rate * along
        relaxed.append(settle(k, keep * h[k] + (even + odd)))
        relaxed.append(settle(k + 1, keep * h[k + 1] + (even - odd)))

    amount = 0.25 * q[0] + 0.125 * ((q[1] + q[2]) + (q[3] + q[4]) + (q[5] + q[6]))
    share = amount * (1.0 / TRACER_RELAX)
    level = share + emission
    drift = share * (4.0 / 3.0)
    rest = 1.0 - 1.0 / TRACER_RELAX

    def trace(k, fluid):
        return jnp.where(solid, q[OPPOSITE[k]], jnp.where(inflow, 0.0, fluid))

    traced = [trace(0, rest * q[0] + level)]
    for k in range(1, TRACE, 2):
        lean = drift * speed[(k - 1) // 2]
        traced.append(trace(k, rest * q[k] + (level + lean)))
        traced.append(trace(k + 1, rest * q[k + 1] + (level - lean)))
    return relaxed, traced


def kernel(
    sizes,
    flow_in,
    trace_in,
    solid_in,
    inflow_in,
    wind_in,
    emission_in,
    flow,
    trace,
    relaxed,
    solid,
    inflow,
    wind,
    emission,
    held,
    x_send,
    x_recv,
    y_send,
    y_recv,
    c_send,
    c_recv,
    in_sem,
    send_sem,
    recv_sem,
):
    rows, width = flow.shape[1], flow.shape[2]
    chunks = width // 128
    gx, gy = lax.axis_index("gx"), lax.axis_index("gy")

    def device(side):
        step_x, step_y = NEIGHBOURS[side]
        return (
            lax.rem(gx + step_x + sizes[0], sizes[0]),
            lax.rem(gy + step_y + sizes[1], sizes[1]),
        )

    barrier = pltpu.get_barrier_semaphore()
    for side in range(8):
        pl.semaphore_signal(barrier, inc=1, device_id=device(side), device_id_type=MESH)

    loads = [
        pltpu.make_async_copy(src, dst, in_sem.at[i])
        for i, (src, dst) in enumerate(
            (
                (flow_in, flow),
                (trace_in, trace),
                (solid_in, solid),
                (inflow_in, inflow),
                (emission_in, emission),
                (wind_in, wind),
            )
        )
    ]
    for load in loads:
        load.start()
    for load in loads:
        load.wait()

    winds = [jnp.concatenate([wind[a : a + 1, :]] * (128 // NZ), axis=1) for a in range(3)]
    for k, state in enumerate(inflow_states(winds)):
        held[k] = jnp.broadcast_to(state, (8, 128))

    def state(k):
        return flow.at[k] if k < FLOW else trace.at[k - FLOW]

    def relax():
        def tile(index, carry):
            row = pl.ds(pl.multiple_of((index // chunks) * 8, 8), 8)
            lane = pl.ds(pl.multiple_of((index % chunks) * 128, 128), 128)
            h = [flow[k, row, lane] for k in range(FLOW)]
            q = [trace[k, row, lane] for k in range(TRACE)]
            settled, traced = relax_cells(
                h,
                q,
                solid[row, lane] == 1,
                inflow[row, lane] == 1,
                emission[row, lane],
                lambda k: held[k],
            )
            for k, cells in enumerate(settled + traced):
                relaxed[k, row, lane] = cells
            return carry

        lax.fori_loop(0, (rows // 8) * chunks, tile, 0)

    height = lax.broadcasted_iota(jnp.int32, (rows, width), 1) % NZ

    def wall(k):
        return 0 if MOVES[k][2] == 1 else NZ - 1

    def stream():
        for k in range(POPS):
            step_x, step_y, step_z = MOVES[k]
            cells = relaxed[k]
            by = step_y * NZ + step_z
            if by != 0:
                cells = pltpu.roll(cells, by % width, 1)
            if step_x != 0:
                cells = pltpu.roll(cells, step_x % rows, 0)
            if step_z != 0:
                cells = jnp.where(height == wall(k), relaxed[BACK[k]], cells)
            state(k)[...] = cells

    lane_group = lax.broadcasted_iota(jnp.int32, (8, 128), 1) // NZ

    def pack(step):
        for side in (0, 1):
            row = 0 if side == 0 else rows - 1
            for i, k in enumerate(SIDES[side]):
                for c in range(chunks):
                    x_send[step, side, pl.ds(i * chunks + c, 1), :] = state(k)[
                        pl.ds(row, 1), pl.ds(c * 128, 128)
                    ]
        for side in (0, 1):
            lane = 0 if side == 0 else width - 128
            group = 0 if side == 0 else 128 // NZ - 1
            pops = SIDES[2 + side]
            for part in range(3):
                columns = []
                for j in range(4):
                    if part < 2:
                        k, top = pops[j], part * 8
                    else:
                        k, top = pops[4 + j % 2], (j // 2) * 8
                    cells = state(k)[pl.ds(top, 8), pl.ds(lane, 128)]
                    by = ((j - group) * NZ) % 128
                    columns.append(pltpu.roll(cells, by, 1) if by else cells)
                cells = columns[3]
                for j in range(3):
                    cells = jnp.where(lane_group == j, columns[j], cells)
                y_send[step, side, pl.ds(part * 8, 8), :] = cells
        for i, k in enumerate(CORNERS):
            row = 0 if MOVES[k][0] == 1 else rows - 1
            lane = 0 if MOVES[k][1] == 1 else width - 128
            c_send[step, i] = state(k)[pl.ds(row, 1), pl.ds(lane, 128)]

    def copies(step):
        pairs = []
        for side in range(8):
            if side < 2:
                src, dst = x_send.at[step, side], x_recv.at[step, side]
            elif side < 4:
                src, dst = y_send.at[step, side - 2], y_recv.at[step, side - 2]
            else:
                src, dst = c_send.at[step, side - 4], c_recv.at[step, side - 4]
            pairs.append(
                pltpu.make_async_remote_copy(
                    src_ref=src,
                    dst_ref=dst,
                    send_sem=send_sem.at[step, side],
                    recv_sem=recv_sem.at[step, side],
                    device_id=device(side),
                    device_id_type=MESH,
                )
            )
        return pairs

    row_height = lax.broadcasted_iota(jnp.int32, (1, 128), 1) % NZ
    tile_height = lax.broadcasted_iota(jnp.int32, (8, 128), 1) % NZ

    def patch(step):
        for side in (0, 1):
            row = 0 if side == 0 else rows - 1
            for i, k in enumerate(SIDES[side]):
                for c in range(chunks):
                    at = (pl.ds(row, 1), pl.ds(c * 128, 128))
                    cells = x_recv[step, side, pl.ds(i * chunks + c, 1), :]
                    if MOVES[k][2] != 0:
                        cells = jnp.where(row_height == wall(k), state(k)[at], cells)
                    state(k)[at] = cells
        for side in (0, 1):
            lane = 0 if side == 0 else width - 128
            group = 0 if side == 0 else 128 // NZ - 1
            for i, k in enumerate(SIDES[2 + side]):
                for half in (0, 1):
                    if i < 4:
                        part, j = half, i
                    else:
                        part, j = 2, 2 * half + i - 4
                    cells = y_recv[step, side, pl.ds(part * 8, 8), :]
                    by = ((group - j) * NZ) % 128
                    if by:
                        cells = pltpu.roll(cells, by, 1)
                    at = (pl.ds(half * 8, 8), pl.ds(lane, 128))
                    take = lane_group == group
                    if MOVES[k][2] != 0:
                        take = take & (tile_height != wall(k))
                    state(k)[at] = jnp.where(take, cells, state(k)[at])
        for i, k in enumerate(CORNERS):
            row = 0 if MOVES[k][0] == 1 else rows - 1
            lane = 0 if MOVES[k][1] == 1 else width - 128
            group = 0 if MOVES[k][1] == 1 else 128 // NZ - 1
            at = (pl.ds(row, 1), pl.ds(lane, 128))
            take = lane_group[:1] == group
            state(k)[at] = jnp.where(take, c_recv[step, i], state(k)[at])

    def advance(step, carry):
        relax()
        stream()
        pack(step)

        @pl.when(step == 0)
        def _():
            pl.semaphore_wait(barrier, 8)

        sent = copies(step)
        for copy in sent:
            copy.start()
        for copy in sent:
            copy.wait()
        patch(step)
        return carry

    lax.fori_loop(0, STEPS, advance, 0)


def local(sizes, populations, tracer, solid_mask, inflow, wind_profile, emission):
    rows, width = solid_mask.shape
    chunks = width // 128
    anywhere = pl.BlockSpec(memory_space=pl.ANY)
    near = pl.BlockSpec(memory_space=pltpu.VMEM)
    side = (STEPS, 2, 6 * chunks, 128)
    column = (STEPS, 2, 24, 128)
    corner = (STEPS, 4, 1, 128)
    return pl.pallas_call(
        functools.partial(kernel, sizes),
        out_shape=(
            jax.ShapeDtypeStruct(populations.shape, jnp.float32),
            jax.ShapeDtypeStruct(tracer.shape, jnp.float32),
        ),
        in_specs=[anywhere] * 6,
        out_specs=(near, near),
        scratch_shapes=[
            pltpu.VMEM((POPS, rows, width), jnp.float32),
            pltpu.VMEM((rows, width), jnp.int32),
            pltpu.VMEM((rows, width), jnp.int32),
            pltpu.VMEM(wind_profile.shape, jnp.float32),
            pltpu.VMEM((rows, width), jnp.float32),
            pltpu.VMEM((FLOW, 8, 128), jnp.float32),
            pltpu.VMEM(side, jnp.float32),
            pltpu.VMEM(side, jnp.float32),
            pltpu.VMEM(column, jnp.float32),
            pltpu.VMEM(column, jnp.float32),
            pltpu.VMEM(corner, jnp.float32),
            pltpu.VMEM(corner, jnp.float32),
            pltpu.SemaphoreType.DMA((6,)),
            pltpu.SemaphoreType.DMA((STEPS, 8)),
            pltpu.SemaphoreType.DMA((STEPS, 8)),
        ],
        compiler_params=pltpu.CompilerParams(collective_id=0, has_side_effects=True),
        name="canyon",
    )(populations, tracer, solid_mask, inflow, wind_profile, emission)


def solution(mesh):
    sizes = (mesh.shape["gx"], mesh.shape["gy"])
    in_specs = (
        P(None, "gx", "gy"),
        P(None, "gx", "gy"),
        P("gx", "gy"),
        P("gx", "gy"),
        P(),
        P("gx", "gy"),
    )
    out_specs = (P(None, "gx", "gy"), P(None, "gx", "gy"))
    return jax.shard_map(
        functools.partial(local, sizes),
        mesh=mesh,
        in_specs=in_specs,
        out_specs=out_specs,
        check_vma=False,
    )
```

time: 109 us -> 51 us (0.47)
  the two profiles are of different devices: /device:TPU:8 before, /device:TPU:1 now
where the time goes in v1:
time: 51 us; the launch traced here: 50.8 us
  Pallas kernels  47.4 us (93%)
  local copies, waits for them, and re-layouts  2.69 us (5%)
  between operations  0.65 us (1%)
    pallas_call x1, Pallas kernels, local(): pl.pallas_call(functools.partial(kernel, sizes), out_shape=(jax.ShapeDtyp...  47.4 us
    unnamed x4, local copies, waits for them, and re-layouts  2.69 us

profile of v1, /device:TPU:1, one launch (start us, length us, event | category | flops | bytes accessed | tf_op | source)
XLA Modules:
  0.0 50.8 jit_solution(3524148877942023498)
XLA Ops:
  0.6 47.4 %canyon.1 = (f32[19,16,512]{2,1,0:T(8,128)}, f32[7,16,512]{2,1,0:T(8,128)}) custom-call(f32[19,16,512]{2,1,0:T(8,128)} %flow_in.1, f32[7,16,512]{2,1,0:T(8,128)} %trace_in.1, s32[16,512]{1,0:T(8,128)} %solid_in.1, s32[16,512]{1,0:T(8,128)} %inflow_in.1, f32[3,32]{1,0:T(4,128)} %wind_in.1, f32[16,512]{1,0:T(8,128)} %emission_in.1), custom_call_target="tpu_custom_call" | custom-call | tf_op jit(solution)/shard_map/canyon/pallas_call | solution.py:352
  48.1 0.0 copy-start
  48.1 2.0 %copy.10 = f32[19,16,512]{2,1,0:T(8,128)} copy(f32[19,16,512]{2,1,0:T(8,128)} %get-tuple-element.4) | data formatting | bytes 1245184
  50.1 0.0 copy-done
  50.1 0.7 %copy.11 = f32[7,16,512]{2,1,0:T(8,128)} copy(f32[7,16,512]{2,1,0:T(8,128)S(1)} %copy-done) | data formatting | bytes 458752
Async XLA Ops:
  48.1 2.0 %copy-start = (f32[7,16,512]{2,1,0:T(8,128)S(1)}, f32[7,16,512]{2,1,0:T(8,128)}, u32[]{:S(2)}) copy-start(f32[7,16,512]{2,1,0:T(8,128)} %get-tuple-element.5) | copy-start | bytes 688132

commit v2 on v1

v2 whole, which is shorter than its diff:
```python
import functools
import math

import jax
import jax.numpy as jnp
from jax import lax
from jax.experimental import pallas as pl
from jax.experimental.pallas import tpu as pltpu
from jax.sharding import PartitionSpec as P

NZ = 32
STEPS = 4
MARGIN = 128
FLOW = 19
TRACE = 7
POPS = FLOW + TRACE

LATTICE = (
    (0, 0, 0),
    (1, 0, 0),
    (-1, 0, 0),
    (0, 1, 0),
    (0, -1, 0),
    (0, 0, 1),
    (0, 0, -1),
    (1, 1, 0),
    (-1, -1, 0),
    (1, -1, 0),
    (-1, 1, 0),
    (1, 0, 1),
    (-1, 0, -1),
    (1, 0, -1),
    (-1, 0, 1),
    (0, 1, 1),
    (0, -1, -1),
    (0, 1, -1),
    (0, -1, 1),
)
OPPOSITE = (0, 2, 1, 4, 3, 6, 5, 8, 7, 10, 9, 12, 11, 14, 13, 16, 15, 18, 17)
MOVES = LATTICE + LATTICE[:TRACE]
BACK = OPPOSITE + tuple(FLOW + k for k in OPPOSITE[:TRACE])
BASE_RELAX = 0.6
SMAGORINSKY = 0.2
TRACER_RELAX = 0.7

PLANES = POPS + 3
SENDS = ((1, 0), (-1, 0), (0, 1), (0, -1), (1, 1), (-1, -1), (1, -1), (-1, 1))
MESH = pl.DeviceIdType.MESH


def layers_of(k, axis, sign):
    if k >= POPS:
        return STEPS - 1
    toward = MOVES[k][axis] * sign
    if toward > 0:
        return STEPS
    if toward == 0:
        return STEPS - 1
    return STEPS - 1 if MOVES[k][2] != 0 else STEPS - 2


def row_units(sign):
    return tuple((k, n) for k in range(PLANES) for n in range(layers_of(k, 0, sign)))


UNITS = {sign: row_units(sign) for sign in (1, -1)}
COUNT = len(UNITS[1])
COLUMN = 128 // NZ


def column_tiles(sign):
    low = sign < 0

    def place(n):
        return n if low else COLUMN - 1 - n

    full = [k for k in range(PLANES) if layers_of(k, 1, sign) == STEPS]
    three = [k for k in range(PLANES) if layers_of(k, 1, sign) == STEPS - 1]
    two = [k for k in range(PLANES) if layers_of(k, 1, sign) == STEPS - 2]
    tiles = []
    for k in full:
        tiles.append({place(n): (k, n) for n in range(STEPS)})
    while three:
        group, three = three[:4], three[4:]
        if len(group) == 4:
            for n in range(3):
                tile = {place(m): (group[n], m) for m in range(3)}
                tile[place(3)] = (group[3], n)
                tiles.append(tile)
        else:
            for k in group:
                tiles.append({place(m): (k, m) for m in range(3)})
    while two:
        group, two = two[:2], two[2:]
        tile = {place(m): (group[0], m) for m in range(2)}
        for k in group[1:]:
            tile.update({place(m + 2): (k, m) for m in range(2)})
        tiles.append(tile)
    return tiles


TILES = {sign: column_tiles(sign) for sign in (1, -1)}
TILE_COUNT = len(TILES[1])


def inflow_states(wind):
    square = wind[0] * wind[0] + wind[1] * wind[1] + wind[2] * wind[2]
    held = []
    for k in range(FLOW):
        along = sum(LATTICE[k][a] * wind[a] for a in range(3) if LATTICE[k][a] != 0)
        held.append(1.0 + 3.0 * along + 4.5 * along * along - 1.5 * square)
    return held


def relax_cells(h, q, solid, inflow, emission, held):
    total = {k: h[k] + h[k + 1] for k in range(1, FLOW, 2)}
    delta = {k: h[k] - h[k + 1] for k in range(1, FLOW, 2)}
    in_xy, in_xz, in_yz = total[7] + total[9], total[11] + total[13], total[15] + total[17]
    along_x, along_y, along_z = 2.0 * total[1], 2.0 * total[3], 2.0 * total[5]
    density = (
        12.0 * h[0] + ((along_x + along_y) + along_z) + ((in_xy + in_xz) + in_yz)
    ) * (1.0 / 36.0)
    speed = [
        (2.0 * delta[1] + (delta[7] + delta[9]) + (delta[11] + delta[13])) * (1.0 / 12.0),
        (2.0 * delta[3] + (delta[7] - delta[9]) + (delta[15] + delta[17])) * (1.0 / 12.0),
        (2.0 * delta[5] + (delta[11] - delta[13]) + (delta[15] - delta[17])) * (1.0 / 12.0),
    ]
    square = [v * v for v in speed]
    third = 3.0 * density
    stress_x = 0.25 * (along_x + in_xy + in_xz) - third - square[0]
    stress_y = 0.25 * (along_y + in_xy + in_yz) - third - square[1]
    stress_z = 0.25 * (along_z + in_xz + in_yz) - third - square[2]
    stress_xy = 0.25 * (total[7] - total[9]) - speed[0] * speed[1]
    stress_xz = 0.25 * (total[11] - total[13]) - speed[0] * speed[2]
    stress_yz = 0.25 * (total[15] - total[17]) - speed[1] * speed[2]
    contraction = (
        stress_x * stress_x
        + stress_y * stress_y
        + stress_z * stress_z
        + 2.0 * (stress_xy * stress_xy + stress_xz * stress_xz + stress_yz * stress_yz)
    )
    gain = 18.0 * math.sqrt(2.0) * SMAGORINSKY * SMAGORINSKY / 9.0
    rate = 2.0 / (
        BASE_RELAX + jnp.sqrt(BASE_RELAX * BASE_RELAX + gain * jnp.sqrt(contraction))
    )
    keep = 1.0 - rate
    base = rate * (density - (square[0] + square[1] + square[2]) * (1.0 / 6.0))
    half = 0.5 * rate

    def settle(k, fluid):
        return jnp.where(solid, h[OPPOSITE[k]], jnp.where(inflow, held(k), fluid))

    relaxed = [settle(0, keep * h[0] + base)]
    for k in range(1, FLOW, 2):
        along = sum(LATTICE[k][a] * speed[a] for a in range(3) if LATTICE[k][a] != 0)
        even = base + half * along * along
        odd = rate * along
        relaxed.append(settle(k, keep * h[k] + (even + odd)))
        relaxed.append(settle(k + 1, keep * h[k + 1] + (even - odd)))

    amount = 0.25 * q[0] + 0.125 * ((q[1] + q[2]) + (q[3] + q[4]) + (q[5] + q[6]))
    share = amount * (1.0 / TRACER_RELAX)
    level = share + emission
    drift = share * (4.0 / 3.0)
    rest = 1.0 - 1.0 / TRACER_RELAX

    def trace(k, fluid):
        return jnp.where(solid, q[OPPOSITE[k]], jnp.where(inflow, 0.0, fluid))

    traced = [trace(0, rest * q[0] + level)]
    for k in range(1, TRACE, 2):
        lean = drift * speed[(k - 1) // 2]
        traced.append(trace(k, rest * q[k] + (level + lean)))
        traced.append(trace(k + 1, rest * q[k + 1] + (level - lean)))
    return relaxed, traced


def plane_of(gx, gy):
    return lax.rem(gx // 2, 2) * 4 + lax.rem(gy, 4)


class Links:
    def __init__(self, sizes, second):
        self.gx, self.gy = lax.axis_index("gx"), lax.axis_index("gy")
        self.sizes = sizes
        here = plane_of(self.gx, self.gy)
        self.out, self.into = [], []
        for side in range(8):
            late_out = self.held_back(here, plane_of(*self.target(side)))
            late_in = self.held_back(plane_of(*self.source(side)), here)
            self.out.append(late_out == second)
            self.into.append(late_in == second)

    @staticmethod
    def held_back(source, target):
        return jnp.where((source <= 4) & (target >= 6), 1, 0)

    def at(self, step_x, step_y):
        return (
            lax.rem(self.gx + step_x + self.sizes[0], self.sizes[0]),
            lax.rem(self.gy + step_y + self.sizes[1], self.sizes[1]),
        )

    def target(self, side):
        return self.at(*SENDS[side])

    def source(self, side):
        return self.at(-SENDS[side][0], -SENDS[side][1])

    def greet(self, barrier):
        for side in range(8):

            @pl.when(self.into[side])
            def _():
                pl.semaphore_signal(
                    barrier, inc=1, device_id=self.source(side), device_id_type=MESH
                )

    def meet(self, barrier):
        count = sum(jnp.where(flag, 1, 0) for flag in self.out)

        @pl.when(count > 0)
        def _():
            pl.semaphore_wait(barrier, count)

    def copy(self, side, boxes_out, boxes_in, sems):
        if side < 2:
            kind, index = 0, side
        elif side < 4:
            kind, index = 1, side - 2
        else:
            kind, index = 2, side - 4
        return pltpu.make_async_remote_copy(
            src_ref=boxes_out[kind].at[index],
            dst_ref=boxes_in[kind].at[index],
            send_sem=sems[0].at[side],
            recv_sem=sems[1].at[side],
            device_id=self.target(side),
            device_id_type=MESH,
        )

    def send(self, sides, boxes_out, boxes_in, sems):
        for side in sides:

            @pl.when(self.out[side])
            def _():
                self.copy(side, boxes_out, boxes_in, sems).start()

    def finish(self, boxes_out, boxes_in, sems):
        for side in range(8):

            @pl.when(self.into[side])
            def _():
                self.copy(side, boxes_out, boxes_in, sems).wait_recv()

        for side in range(8):

            @pl.when(self.out[side])
            def _():
                self.copy(side, boxes_out, boxes_in, sems).wait_send()


def inflow_tiles(wind, held):
    winds = [jnp.concatenate([wind[a : a + 1, :]] * COLUMN, axis=1) for a in range(3)]
    for k, cells in enumerate(inflow_states(winds)):
        held[k] = jnp.broadcast_to(cells, (8, 128))


def exchange_first(
    sizes,
    flow_in,
    trace_in,
    solid_in,
    inflow_in,
    wind_in,
    emission_in,
    relaxed,
    x_out,
    y_out,
    c_out,
    x_got,
    y_got,
    c_got,
    held,
    flow,
    trace,
    solid,
    inflow,
    wind,
    in_sem,
    send_sem,
    recv_sem,
):
    rows, width = solid.shape
    chunks = width // 128
    links = Links(sizes, 0)
    barrier = pltpu.get_barrier_semaphore()
    links.greet(barrier)

    loads = [
        pltpu.make_async_copy(src, dst, in_sem.at[i])
        for i, (src, dst) in enumerate(
            (
                (flow_in, flow),
                (trace_in, trace),
                (solid_in, solid),
                (inflow_in, inflow),
                (emission_in, relaxed.at[PLANES - 1]),
                (wind_in, wind),
            )
        )
    ]
    for load in loads:
        load.start()
    for load in loads:
        load.wait()
    inflow_tiles(wind, held)

    def tile(index, carry):
        row = pl.ds(pl.multiple_of((index // chunks) * 8, 8), 8)
        lane = pl.ds(pl.multiple_of((index % chunks) * 128, 128), 128)
        is_solid = solid[row, lane] == 1
        is_inflow = inflow[row, lane] == 1
        settled, traced = relax_cells(
            [flow[k, row, lane] for k in range(FLOW)],
            [trace[k, row, lane] for k in range(TRACE)],
            is_solid,
            is_inflow,
            relaxed[PLANES - 1, row, lane],
            lambda k: held[k],
        )
        for k, cells in enumerate(settled + traced):
            relaxed[k, row, lane] = cells
        relaxed[POPS, row, lane] = jnp.where(is_solid, 1.0, 0.0)
        relaxed[POPS + 1, row, lane] = jnp.where(is_inflow, 1.0, 0.0)
        return carry

    lax.fori_loop(0, (rows // 8) * chunks, tile, 0)

    def layer_row(sign, n):
        return rows - 1 - n if sign > 0 else n

    boxes_out, boxes_in = (x_out, y_out, c_out), (x_got, y_got, c_got)
    sems = (send_sem, recv_sem)

    for i, (sign_x, sign_y) in enumerate(SENDS[4:]):
        lane = width - 128 if sign_y > 0 else 0
        for u, (k, n) in enumerate(UNITS[sign_x]):
            c_out[i, pl.ds(u, 1), :] = relaxed[
                k, pl.ds(layer_row(sign_x, n), 1), pl.ds(lane, 128)
            ]
    links.meet(barrier)
    links.send(range(4, 8), boxes_out, boxes_in, sems)

    for i, sign in enumerate((1, -1)):
        for u, (k, n) in enumerate(UNITS[sign]):
            for c in range(chunks):
                x_out[i, pl.ds(u * chunks + c, 1), :] = relaxed[
                    k, pl.ds(layer_row(sign, n), 1), pl.ds(c * 128, 128)
                ]
    links.send((0, 1), boxes_out, boxes_in, sems)

    group = lax.broadcasted_iota(jnp.int32, (8, 128), 1) // NZ
    for i, sign in enumerate((1, -1)):
        lane = width - 128 if sign > 0 else 0
        for t, tile_map in enumerate(TILES[sign]):
            for top in range(0, rows, 8):
                parts = {}
                for place, (k, n) in tile_map.items():
                    own = COLUMN - 1 - n if sign > 0 else n
                    parts.setdefault((k, (place - own) * NZ % 128), []).append(place)
                cells = None
                for (k, by), places in parts.items():
                    piece = relaxed[k, pl.ds(top, 8), pl.ds(lane, 128)]
                    if by:
                        piece = pltpu.roll(piece, by, 1)
                    if cells is None:
                        cells = piece
                    else:
                        take = functools.reduce(jnp.logical_or, [group == p for p in places])
                        cells = jnp.where(take, piece, cells)
                y_out[i, pl.ds(t * rows + top, 8), :] = cells
    links.send((2, 3), boxes_out, boxes_in, sems)
    links.finish(boxes_out, boxes_in, sems)


def exchange_second(
    sizes, x_out, y_out, c_out, x_got, y_got, c_got, send_sem, recv_sem
):
    links = Links(sizes, 1)
    barrier = pltpu.get_barrier_semaphore()
    boxes_out, boxes_in = (x_out, y_out, c_out), (x_got, y_got, c_got)
    sems = (send_sem, recv_sem)
    links.greet(barrier)
    links.meet(barrier)
    links.send(range(8), boxes_out, boxes_in, sems)
    links.finish(boxes_out, boxes_in, sems)


def compute(
    sizes,
    relaxed_in,
    held,
    x_one,
    y_one,
    c_one,
    x_two,
    y_two,
    c_two,
    flow,
    trace,
    grown,
    state,
):
    rows, width = flow.shape[1], flow.shape[2]
    chunks = width // 128
    tall, wide = rows + 2 * STEPS, width + 2 * MARGIN
    early = Links(sizes, 0).into

    def center(k, carry):
        grown[k, pl.ds(STEPS, rows), pl.ds(MARGIN, width)] = relaxed_in[k]
        return carry

    lax.fori_loop(0, PLANES, center, 0)

    def layer_row(sign, n):
        return STEPS - 1 - n if sign > 0 else STEPS + rows + n

    def from_either(flag, unpack, one, two):
        @pl.when(flag)
        def _():
            unpack(one)

        @pl.when(jnp.logical_not(flag))
        def _():
            unpack(two)

    for i, sign in enumerate((1, -1)):

        def rows_from(box, i=i, sign=sign):
            for u, (k, n) in enumerate(UNITS[sign]):
                for c in range(chunks):
                    grown[k, pl.ds(layer_row(sign, n), 1), pl.ds(MARGIN + c * 128, 128)] = box[
                        i, pl.ds(u * chunks + c, 1), :
                    ]

        from_either(early[i], rows_from, x_one, x_two)

    group = lax.broadcasted_iota(jnp.int32, (8, 128), 1) // NZ
    for i, sign in enumerate((1, -1)):
        lane = 0 if sign > 0 else MARGIN + width

        def columns_from(box, i=i, sign=sign, lane=lane):
            pieces = {}
            for t, tile_map in enumerate(TILES[sign]):
                for place, (k, n) in tile_map.items():
                    own = COLUMN - 1 - n if sign > 0 else n
                    pieces.setdefault(k, {}).setdefault((t, (own - place) * NZ % 128), []).append(
                        own
                    )
            for k, parts in pieces.items():
                for top in range(0, rows, 8):
                    cells = None
                    for (t, by), places in parts.items():
                        piece = box[i, pl.ds(t * rows + top, 8), :]
                        if by:
                            piece = pltpu.roll(piece, by, 1)
                        if cells is None:
                            cells = piece
                        else:
                            take = functools.reduce(jnp.logical_or, [group == p for p in places])
                            cells = jnp.where(take, piece, cells)
                    grown[k, pl.ds(STEPS + top, 8), pl.ds(lane, 128)] = cells

        from_either(early[2 + i], columns_from, y_one, y_two)

    for i, (sign_x, sign_y) in enumerate(SENDS[4:]):
        lane = 0 if sign_y > 0 else MARGIN + width

        def corner_from(box, i=i, sign_x=sign_x, lane=lane):
            for u, (k, n) in enumerate(UNITS[sign_x]):
                grown[k, pl.ds(layer_row(sign_x, n), 1), pl.ds(lane, 128)] = box[
                    i, pl.ds(u, 1), :
                ]

        from_either(early[4 + i], corner_from, c_one, c_two)

    height = lax.broadcasted_iota(jnp.int32, (tall, wide), 1) % NZ

    def passed(k, up):
        step_x, step_y, step_z = MOVES[k]
        cells = grown[k]
        by = (step_y * NZ + step_z) % wide
        if by:
            cells = pltpu.roll(cells, by, 1)
        if step_x - up:
            cells = pltpu.roll(cells, (step_x - up) % tall, 0)
        if step_z:
            back = grown[BACK[k]]
            if up:
                back = pltpu.roll(back, (-up) % tall, 0)
            cells = jnp.where(height == (0 if step_z == 1 else NZ - 1), back, cells)
        return cells

    across = wide // 128

    def tile(index, carry):
        row = pl.ds(pl.multiple_of((index // across) * 8, 8), 8)
        lane = pl.ds(pl.multiple_of((index % across) * 128, 128), 128)
        settled, traced = relax_cells(
            [state[k, row, lane] for k in range(FLOW)],
            [state[FLOW + k, row, lane] for k in range(TRACE)],
            grown[POPS, row, lane] == 1.0,
            grown[POPS + 1, row, lane] == 1.0,
            grown[POPS + 2, row, lane],
            lambda k: held[k],
        )
        for k, cells in enumerate(settled + traced):
            grown[k, row, lane] = cells
        return carry

    def step(_, carry):
        for k in range(POPS):
            state[k] = passed(k, 0)
        lax.fori_loop(0, (tall // 8) * across, tile, 0)
        return carry

    lax.fori_loop(0, STEPS - 1, step, 0)
    for k in range(POPS):
        cells = passed(k, STEPS)[:rows, MARGIN : MARGIN + width]
        if k < FLOW:
            flow[k] = cells
        else:
            trace[k - FLOW] = cells


def local(sizes, populations, tracer, solid_mask, inflow, wind_profile, emission):
    rows, width = solid_mask.shape
    chunks = width // 128
    far = pl.BlockSpec(memory_space=pltpu.HBM)
    near = pl.BlockSpec(memory_space=pltpu.VMEM)
    boxes = (
        pltpu.VMEM((2, COUNT * chunks, 128), jnp.float32),
        pltpu.VMEM((2, TILE_COUNT * rows, 128), jnp.float32),
        pltpu.VMEM((4, COUNT, 128), jnp.float32),
    )

    def held_near(arrays):
        return [pltpu.with_memory_space_constraint(a, pltpu.VMEM) for a in arrays]

    held_far = [
        pltpu.with_memory_space_constraint(a, pltpu.HBM)
        for a in (populations, tracer, solid_mask, inflow, wind_profile, emission)
    ]
    relaxed, *first, held = pl.pallas_call(
        functools.partial(exchange_first, sizes),
        out_shape=(pltpu.VMEM((PLANES, rows, width), jnp.float32),)
        + boxes
        + boxes
        + (pltpu.VMEM((FLOW, 8, 128), jnp.float32),),
        in_specs=[far] * 6,
        out_specs=(near,) * 8,
        scratch_shapes=[
            pltpu.VMEM(populations.shape, jnp.float32),
            pltpu.VMEM(tracer.shape, jnp.float32),
            pltpu.VMEM((rows, width), jnp.int32),
            pltpu.VMEM((rows, width), jnp.int32),
            pltpu.VMEM(wind_profile.shape, jnp.float32),
            pltpu.SemaphoreType.DMA((6,)),
            pltpu.SemaphoreType.DMA((8,)),
            pltpu.SemaphoreType.DMA((8,)),
        ],
        compiler_params=pltpu.CompilerParams(collective_id=0, has_side_effects=True, vmem_limit_bytes=16 << 20),
        name="first",
    )(*held_far)
    second = pl.pallas_call(
        functools.partial(exchange_second, sizes),
        out_shape=boxes,
        in_specs=[near] * 3,
        out_specs=(near,) * 3,
        scratch_shapes=[pltpu.SemaphoreType.DMA((8,)), pltpu.SemaphoreType.DMA((8,))],
        compiler_params=pltpu.CompilerParams(collective_id=1, has_side_effects=True, vmem_limit_bytes=8 << 20),
        name="second",
    )(*held_near(first[:3]))
    tall, wide = rows + 2 * STEPS, width + 2 * MARGIN
    return pl.pallas_call(
        functools.partial(compute, sizes),
        out_shape=(
            jax.ShapeDtypeStruct(populations.shape, jnp.float32),
            jax.ShapeDtypeStruct(tracer.shape, jnp.float32),
        ),
        in_specs=[near] * 8,
        out_specs=(near, near),
        scratch_shapes=[
            pltpu.VMEM((PLANES, tall, wide), jnp.float32),
            pltpu.VMEM((POPS, tall, wide), jnp.float32),
        ],
        compiler_params=pltpu.CompilerParams(vmem_limit_bytes=24 << 20),
        name="compute",
    )(*held_near([relaxed, held, *first[3:], *second]))


def solution(mesh):
    sizes = (mesh.shape["gx"], mesh.shape["gy"])
    in_specs = (
        P(None, "gx", "gy"),
        P(None, "gx", "gy"),
        P("gx", "gy"),
        P("gx", "gy"),
        P(),
        P("gx", "gy"),
    )
    out_specs = (P(None, "gx", "gy"), P(None, "gx", "gy"))
    return jax.shard_map(
        functools.partial(local, sizes),
        mesh=mesh,
        in_specs=in_specs,
        out_specs=out_specs,
        check_vma=False,
    )
```

time: 51 us -> 52.1 us (1.022)
  Pallas kernels: 47.4 us -> 51.3 us
  local copies, waits for them, and re-layouts: 2.69 us -> 0 us
    pallas_call x1 -> x3, Pallas kernels: 47.4 us -> 51.3 us  [the longest x1 36.9 us: local(): pl.pallas_call(functools.partial(exchange_first, sizes), out_shape=(pltpu...]
    unnamed x4 -> x0, local copies, waits for them, and re-layouts: 2.69 us -> none
where the time goes in v2:
time: 52.1 us; the launch traced here: 51.9 us
  Pallas kernels  51.3 us (98%)
  between operations  0.65 us (1%)
    pallas_call x1, Pallas kernels, local(): pl.pallas_call(functools.partial(exchange_first, sizes), out_shape=(pltpu...  36.9 us
    pallas_call x1, Pallas kernels, local(): pl.pallas_call(functools.partial(compute, sizes), out_shape=(jax.ShapeDty...  7.39 us
    pallas_call x1, Pallas kernels, local(): pl.pallas_call(functools.partial(exchange_second, sizes), out_shape=boxes...  6.98 us

profile of v2, /device:TPU:1, one launch (start us, length us, event | category | flops | bytes accessed | tf_op | source)
XLA Modules:
  0.0 51.9 jit_solution(14664627946176287861)
XLA Ops:
  0.6 36.9 %first.1 = (f32[29,16,512]{2,1,0:T(8,128)S(1)}, f32[2,356,128]{2,1,0:T(8,128)S(1)}, f32[2,368,128]{2,1,0:T(8,128)S(1)}, f32[4,89,128]{2,1,0:T(8,128)S(1)}, f32[2...) custom-call(f32[19,16,512]{2,1,0:T(8,128)} %flow_in.1, ...), custom_call_target="tpu_custom_call" | custom-call | tf_op jit(solution)/shard_map/first/pallas_call | solution.py:555
  37.6 7.0 %second.1 = (f32[2,356,128]{2,1,0:T(8,128)S(1)}, f32[2,368,128]{2,1,0:T(8,128)S(1)}, f32[4,89,128]{2,1,0:T(8,128)S(1)}) custom-call(f32[2,356,128]{2,1,0:T(8,128)S(1)} %get-tuple-element.18.x_out, f32[2,368,128]{2,1,0:T(8,128)S(1)} %get-tuple-element.19.y_out, f32[4,89,128]{2,1,0:T(8,128)S(1)} %get-tuple-element.20.c_out), custom_call_target="tpu_custom_call" | custom-call | tf_op jit(solution)/shard_map/second/pallas_call | solution.py:576
  44.6 7.4 %compute.1 = (f32[19,16,512]{2,1,0:T(8,128)}, f32[7,16,512]{2,1,0:T(8,128)}) custom-call(f32[29,16,512]{2,1,0:T(8,128)S(1)} %get-tuple-element.13.relaxed_in, f32[19,8,128]{2,1,0:T(8,128)S(1)} %get-tuple-element.14.held, f32[2,356,128]{2,1,0:T(8,128)S(1)} %get-tuple-element.15.x_one, f32[2,368,128]{2,1,0:T(8,128)S(1)} %get-tuple-element.16.y_one, ...), custom_call_target="tpu_custom_call" | custom-call | tf_op jit(solution)/shard_map/compute/pallas_call | solution.py:586

commit v3 on v1

v3 whole, which is shorter than its diff:
```python
import functools
import math

import jax
import jax.numpy as jnp
from jax import lax
from jax.experimental import pallas as pl
from jax.experimental.pallas import tpu as pltpu
from jax.sharding import PartitionSpec as P

NZ = 32
STEPS = 4
FLOW = 19
TRACE = 7
POPS = FLOW + TRACE

LATTICE = (
    (0, 0, 0),
    (1, 0, 0),
    (-1, 0, 0),
    (0, 1, 0),
    (0, -1, 0),
    (0, 0, 1),
    (0, 0, -1),
    (1, 1, 0),
    (-1, -1, 0),
    (1, -1, 0),
    (-1, 1, 0),
    (1, 0, 1),
    (-1, 0, -1),
    (1, 0, -1),
    (-1, 0, 1),
    (0, 1, 1),
    (0, -1, -1),
    (0, 1, -1),
    (0, -1, 1),
)
OPPOSITE = (0, 2, 1, 4, 3, 6, 5, 8, 7, 10, 9, 12, 11, 14, 13, 16, 15, 18, 17)
MOVES = LATTICE + LATTICE[:TRACE]
BACK = OPPOSITE + tuple(FLOW + k for k in OPPOSITE[:TRACE])
BASE_RELAX = 0.6
SMAGORINSKY = 0.2
TRACER_RELAX = 0.7

PLANES = POPS + 3
DEPTH = 2
ROUNDS = STEPS // DEPTH
SENDS = ((1, 0), (-1, 0), (0, 1), (0, -1), (1, 1), (-1, -1), (1, -1), (-1, 1))
MESH = pl.DeviceIdType.MESH
GROUPS = 128 // NZ
ROW_MARGIN = 8
LANE_MARGIN = 128


def layers_of(k, axis, sign):
    if k >= POPS:
        return DEPTH - 1
    toward = MOVES[k][axis] * sign
    if toward > 0:
        return DEPTH
    if toward == 0:
        return DEPTH - 1
    return DEPTH - 1 if MOVES[k][2] != 0 else DEPTH - 2


def row_units(planes, sign):
    return [(k, n) for k in range(planes) for n in range(layers_of(k, 0, sign))]


def column_units(planes, sign):
    pairs = [k for k in range(planes) if layers_of(k, 1, sign) == DEPTH]
    singles = [k for k in range(planes) if layers_of(k, 1, sign) == DEPTH - 1]
    return [(k, n) for k in pairs for n in range(DEPTH)] + [(k, 0) for k in singles]


def corner_units(planes, sign_x, sign_y):
    units = [
        (k, n, m)
        for k in range(planes)
        for n in range(layers_of(k, 0, sign_x))
        for m in range(layers_of(k, 1, sign_y))
    ]
    near = [u for u in units if u[2] == 0]
    far = [u for u in units if u[2] == 1]
    height = -(-len(near) // 3)
    return height, [near[:height], near[height : 2 * height], near[2 * height :], far]


ROWS_OF = [len(row_units(p, 1)) for p in (PLANES, POPS)]
TILES_OF = [-(-len(column_units(p, 1)) // GROUPS) for p in (PLANES, POPS)]
CORNER_OF = [corner_units(p, 1, 1)[0] for p in (PLANES, POPS)]


def inflow_states(wind):
    square = wind[0] * wind[0] + wind[1] * wind[1] + wind[2] * wind[2]
    held = []
    for k in range(FLOW):
        along = sum(LATTICE[k][a] * wind[a] for a in range(3) if LATTICE[k][a] != 0)
        held.append(1.0 + 3.0 * along + 4.5 * along * along - 1.5 * square)
    return held


def relax_cells(h, q, solid, inflow, emission, held):
    total = {k: h[k] + h[k + 1] for k in range(1, FLOW, 2)}
    delta = {k: h[k] - h[k + 1] for k in range(1, FLOW, 2)}
    in_xy, in_xz, in_yz = total[7] + total[9], total[11] + total[13], total[15] + total[17]
    along_x, along_y, along_z = 2.0 * total[1], 2.0 * total[3], 2.0 * total[5]
    density = (
        12.0 * h[0] + ((along_x + along_y) + along_z) + ((in_xy + in_xz) + in_yz)
    ) * (1.0 / 36.0)
    speed = [
        (2.0 * delta[1] + (delta[7] + delta[9]) + (delta[11] + delta[13])) * (1.0 / 12.0),
        (2.0 * delta[3] + (delta[7] - delta[9]) + (delta[15] + delta[17])) * (1.0 / 12.0),
        (2.0 * delta[5] + (delta[11] - delta[13]) + (delta[15] - delta[17])) * (1.0 / 12.0),
    ]
    square = [v * v for v in speed]
    third = 3.0 * density
    stress_x = 0.25 * (along_x + in_xy + in_xz) - third - square[0]
    stress_y = 0.25 * (along_y + in_xy + in_yz) - third - square[1]
    stress_z = 0.25 * (along_z + in_xz + in_yz) - third - square[2]
    stress_xy = 0.25 * (total[7] - total[9]) - speed[0] * speed[1]
    stress_xz = 0.25 * (total[11] - total[13]) - speed[0] * speed[2]
    stress_yz = 0.25 * (total[15] - total[17]) - speed[1] * speed[2]
    contraction = (
        stress_x * stress_x
        + stress_y * stress_y
        + stress_z * stress_z
        + 2.0 * (stress_xy * stress_xy + stress_xz * stress_xz + stress_yz * stress_yz)
    )
    gain = 18.0 * math.sqrt(2.0) * SMAGORINSKY * SMAGORINSKY / 9.0
    rate = 2.0 / (
        BASE_RELAX + jnp.sqrt(BASE_RELAX * BASE_RELAX + gain * jnp.sqrt(contraction))
    )
    keep = 1.0 - rate
    base = rate * (density - (square[0] + square[1] + square[2]) * (1.0 / 6.0))
    half = 0.5 * rate

    def settle(k, fluid):
        return jnp.where(solid, h[OPPOSITE[k]], jnp.where(inflow, held(k), fluid))

    relaxed = [settle(0, keep * h[0] + base)]
    for k in range(1, FLOW, 2):
        along = sum(LATTICE[k][a] * speed[a] for a in range(3) if LATTICE[k][a] != 0)
        even = base + half * along * along
        odd = rate * along
        relaxed.append(settle(k, keep * h[k] + (even + odd)))
        relaxed.append(settle(k + 1, keep * h[k + 1] + (even - odd)))

    amount = 0.25 * q[0] + 0.125 * ((q[1] + q[2]) + (q[3] + q[4]) + (q[5] + q[6]))
    share = amount * (1.0 / TRACER_RELAX)
    level = share + emission
    drift = share * (4.0 / 3.0)
    rest = 1.0 - 1.0 / TRACER_RELAX

    def trace(k, fluid):
        return jnp.where(solid, q[OPPOSITE[k]], jnp.where(inflow, 0.0, fluid))

    traced = [trace(0, rest * q[0] + level)]
    for k in range(1, TRACE, 2):
        lean = drift * speed[(k - 1) // 2]
        traced.append(trace(k, rest * q[k] + (level + lean)))
        traced.append(trace(k + 1, rest * q[k + 1] + (level - lean)))
    return relaxed, traced


def exchange(
    sizes,
    flow_in,
    trace_in,
    solid_in,
    inflow_in,
    wind_in,
    emission_in,
    relaxed,
    state,
    solid,
    inflow,
    wind,
    held,
    stage,
    in_sem,
    send_sem,
    recv_sem,
    *boxes,
):
    rows, width = solid.shape
    chunks = width // 128
    tall, wide = rows + ROW_MARGIN, width + LANE_MARGIN
    gx, gy = lax.axis_index("gx"), lax.axis_index("gy")

    def device(side):
        step_x, step_y = SENDS[side]
        return (
            lax.rem(gx + step_x + sizes[0], sizes[0]),
            lax.rem(gy + step_y + sizes[1], sizes[1]),
        )

    barrier = pltpu.get_barrier_semaphore()
    for side in range(8):
        pl.semaphore_signal(barrier, inc=1, device_id=device(side), device_id_type=MESH)

    block = (slice(None), pl.ds(0, rows), pl.ds(0, width))
    loads = [
        pltpu.make_async_copy(source, target, in_sem.at[i])
        for i, (source, target) in enumerate(
            (
                (flow_in, state.at[pl.ds(0, FLOW), pl.ds(0, rows), pl.ds(0, width)]),
                (trace_in, state.at[pl.ds(FLOW, TRACE), pl.ds(0, rows), pl.ds(0, width)]),
                (solid_in, solid),
                (inflow_in, inflow),
                (emission_in, relaxed.at[PLANES - 1, pl.ds(0, rows), pl.ds(0, width)]),
                (wind_in, wind),
            )
        )
    ]
    for load in loads:
        load.start()
    for load in loads:
        load.wait()
    winds = [jnp.concatenate([wind[a : a + 1, :]] * GROUPS, axis=1) for a in range(3)]
    for k, cells in enumerate(inflow_states(winds)):
        held[k] = jnp.broadcast_to(cells, (8, 128))
    relaxed[POPS, pl.ds(0, rows), pl.ds(0, width)] = jnp.where(solid[...] == 1, 1.0, 0.0)
    relaxed[POPS + 1, pl.ds(0, rows), pl.ds(0, width)] = jnp.where(inflow[...] == 1, 1.0, 0.0)

    def relax(row_tiles, lane_tiles):
        def tile(index, carry):
            row = pl.ds(pl.multiple_of((index // lane_tiles) * 8, 8), 8)
            lane = pl.ds(pl.multiple_of((index % lane_tiles) * 128, 128), 128)
            settled, traced = relax_cells(
                [state[k, row, lane] for k in range(FLOW)],
                [state[FLOW + k, row, lane] for k in range(TRACE)],
                relaxed[POPS, row, lane] == 1.0,
                relaxed[POPS + 1, row, lane] == 1.0,
                relaxed[POPS + 2, row, lane],
                lambda k: held[k],
            )
            for k, cells in enumerate(settled + traced):
                relaxed[k, row, lane] = cells
            return carry

        lax.fori_loop(0, row_tiles * lane_tiles, tile, 0)

    group = lax.broadcasted_iota(jnp.int32, (8, 128), 1) // NZ

    def merge(pieces):
        cells = pieces[0][0]
        for piece, places in pieces[1:]:
            take = functools.reduce(jnp.logical_or, [group == p for p in places])
            cells = jnp.where(take, piece, cells)
        return cells

    def turned(piece, by):
        by = by * NZ % 128
        return pltpu.roll(piece, by, 1) if by else piece

    def pack_corners(planes, box):
        for i, (sign_x, sign_y) in enumerate(SENDS[4:]):
            lane = width - 128 if sign_y > 0 else 0
            height, places = corner_units(planes, sign_x, sign_y)
            for j, units in enumerate(places):
                for u, (k, n, m) in enumerate(units):
                    row = rows - 1 - n if sign_x > 0 else n
                    stage[i, j, pl.ds(u, 1), :] = relaxed[k, pl.ds(row, 1), pl.ds(lane, 128)]
            for top in range(0, height, 8):
                pieces = []
                for j in range(4):
                    m = 1 if j == 3 else 0
                    own = GROUPS - 1 - m if sign_y > 0 else m
                    pieces.append((turned(stage[i, j, pl.ds(top, 8), :], j - own), [j]))
                count = min(8, height - top)
                box[i, pl.ds(top, count), :] = merge(pieces)[:count]

    def pack_rows(planes, box):
        for i, sign in enumerate((1, -1)):
            for u, (k, n) in enumerate(row_units(planes, sign)):
                row = rows - 1 - n if sign > 0 else n
                for c in range(chunks):
                    box[i, pl.ds(u * chunks + c, 1), :] = relaxed[
                        k, pl.ds(row, 1), pl.ds(c * 128, 128)
                    ]

    def pack_columns(planes, box):
        for i, sign in enumerate((1, -1)):
            lane = width - 128 if sign > 0 else 0
            units = column_units(planes, sign)
            for t in range(0, len(units), GROUPS):
                parts = {}
                for place, (k, n) in enumerate(units[t : t + GROUPS]):
                    own = GROUPS - 1 - n if sign > 0 else n
                    parts.setdefault((k, place - own), []).append(place)
                for top in range(0, rows, 8):
                    box[i, pl.ds(t // GROUPS * rows + top, 8), :] = merge(
                        [
                            (turned(relaxed[k, pl.ds(top, 8), pl.ds(lane, 128)], by), places)
                            for (k, by), places in parts.items()
                        ]
                    )

    def unpack_rows(planes, box):
        for i, sign in enumerate((1, -1)):
            for u, (k, n) in enumerate(row_units(planes, sign)):
                row = tall - 1 - n if sign > 0 else rows + n
                for c in range(chunks):
                    relaxed[k, pl.ds(row, 1), pl.ds(c * 128, 128)] = box[
                        i, pl.ds(u * chunks + c, 1), :
                    ]

    def unpack_columns(planes, box):
        for top in range(0, rows, 8):
            for k in range(planes):
                parts = {}
                for i, sign in enumerate((1, -1)):
                    units = column_units(planes, sign)
                    for n in range(layers_of(k, 1, sign)):
                        u = units.index((k, n))
                        own = GROUPS - 1 - n if sign > 0 else n
                        parts.setdefault((i, u // GROUPS, own - u % GROUPS), []).append(own)
                relaxed[k, pl.ds(top, 8), pl.ds(width, 128)] = merge(
                    [
                        (turned(box[i, pl.ds(t * rows + top, 8), :], by), places)
                        for (i, t, by), places in parts.items()
                    ]
                )

    def unpack_corners(planes, box):
        for i, (sign_x, sign_y) in enumerate(SENDS[4:]):
            height, places = corner_units(planes, sign_x, sign_y)
            for j, units in enumerate(places):
                m = 1 if j == 3 else 0
                own = GROUPS - 1 - m if sign_y > 0 else m
                for top in range(0, len(units), 8):
                    count = min(8, height - top)
                    stage[i, j, pl.ds(top, count), :] = turned(
                        box[i, pl.ds(top, count), :], own - j
                    )
                for u, (k, n, _) in enumerate(units):
                    row = tall - 1 - n if sign_x > 0 else rows + n
                    at = (k, pl.ds(row, 1), pl.ds(width, 128))
                    relaxed[at] = jnp.where(
                        group[:1] == own, stage[i, j, pl.ds(u, 1), :], relaxed[at]
                    )

    height = lax.broadcasted_iota(jnp.int32, (tall, wide), 1) % NZ

    def copies(step):
        x_out, x_got, y_out, y_got, c_out, c_got = boxes[6 * step : 6 * step + 6]
        pairs = []
        for side in range(8):
            if side < 2:
                source, target = x_out.at[side], x_got.at[side]
            elif side < 4:
                source, target = y_out.at[side - 2], y_got.at[side - 2]
            else:
                source, target = c_out.at[side - 4], c_got.at[side - 4]
            pairs.append(
                pltpu.make_async_remote_copy(
                    src_ref=source,
                    dst_ref=target,
                    send_sem=send_sem.at[step, side],
                    recv_sem=recv_sem.at[step, side],
                    device_id=device(side),
                    device_id_type=MESH,
                )
            )
        return pairs

    for step in range(ROUNDS):
        planes = POPS if step else PLANES
        x_out, x_got, y_out, y_got, c_out, c_got = boxes[6 * step : 6 * step + 6]
        sent = copies(step)
        relax(rows // 8, chunks)
        pack_rows(planes, x_out)
        if step == 0:
            pl.semaphore_wait(barrier, 8)
        for side in (0, 1):
            sent[side].start()
        pack_corners(planes, c_out)
        for side in range(4, 8):
            sent[side].start()
        pack_columns(planes, y_out)
        for side in (2, 3):
            sent[side].start()
        for side in (2, 3):
            sent[side].wait_recv()
        unpack_columns(planes, y_got)
        for side in (4, 5, 6, 7):
            sent[side].wait_recv()
        unpack_corners(planes, c_got)
        for side in (0, 1):
            sent[side].wait_recv()
        unpack_rows(planes, x_got)
        for copy in sent:
            copy.wait_send()
        for k in range(POPS):
            state[k] = passed(relaxed, k, height)
        relax(tall // 8, wide // 128)
        if step < ROUNDS - 1:
            for k in range(POPS):
                state[k, pl.ds(0, rows), pl.ds(0, width)] = passed(relaxed, k, height)[
                    :rows, :width
                ]


def passed(relaxed, k, height):
    step_x, step_y, step_z = MOVES[k]
    tall, wide = height.shape
    cells = relaxed[k]
    by = (step_y * NZ + step_z) % wide
    if by:
        cells = pltpu.roll(cells, by, 1)
    if step_x:
        cells = pltpu.roll(cells, step_x % tall, 0)
    if step_z:
        cells = jnp.where(height == (0 if step_z == 1 else NZ - 1), relaxed[BACK[k]], cells)
    return cells


def finish(relaxed, flow_out, trace_out, flow, trace, out_sem):
    rows, width = flow.shape[1:]
    height = lax.broadcasted_iota(jnp.int32, relaxed.shape[1:], 1) % NZ
    writes = []
    for k in range(POPS):
        near, far, at = (flow, flow_out, k) if k < FLOW else (trace, trace_out, k - FLOW)
        near[at] = passed(relaxed, k, height)[:rows, :width]
        writes.append(pltpu.make_async_copy(near.at[at], far.at[at], out_sem.at[k]))
        if k:
            writes[k - 1].start()
    writes[POPS - 1].start()
    for write in writes:
        write.wait()


def local(sizes, populations, tracer, solid_mask, inflow, wind_profile, emission):
    rows, width = solid_mask.shape
    chunks = width // 128
    tall, wide = rows + ROW_MARGIN, width + LANE_MARGIN
    far = pl.BlockSpec(memory_space=pltpu.HBM)
    near = pl.BlockSpec(memory_space=pltpu.VMEM)
    boxes = []
    for step in range(ROUNDS):
        kind = 1 if step else 0
        for shape in (
            (2, ROWS_OF[kind] * chunks, 128),
            (2, TILES_OF[kind] * rows, 128),
            (4, CORNER_OF[kind], 128),
        ):
            boxes += [pltpu.VMEM(shape, jnp.float32)] * 2
    held_far = [
        pltpu.with_memory_space_constraint(a, pltpu.HBM)
        for a in (populations, tracer, solid_mask, inflow, wind_profile, emission)
    ]
    relaxed = pl.pallas_call(
        functools.partial(exchange, sizes),
        out_shape=pltpu.VMEM((PLANES, tall, wide), jnp.float32),
        in_specs=[far] * 6,
        out_specs=near,
        scratch_shapes=[
            pltpu.VMEM((POPS, tall, wide), jnp.float32),
            pltpu.VMEM((rows, width), jnp.int32),
            pltpu.VMEM((rows, width), jnp.int32),
            pltpu.VMEM(wind_profile.shape, jnp.float32),
            pltpu.VMEM((FLOW, 8, 128), jnp.float32),
            pltpu.VMEM((4, 4, 16, 128), jnp.float32),
            pltpu.SemaphoreType.DMA((6,)),
            pltpu.SemaphoreType.DMA((ROUNDS, 8)),
            pltpu.SemaphoreType.DMA((ROUNDS, 8)),
            *boxes,
        ],
        compiler_params=pltpu.CompilerParams(
            collective_id=0, has_side_effects=True, vmem_limit_bytes=24 << 20
        ),
        name="exchange",
    )(*held_far)
    return pl.pallas_call(
        finish,
        out_shape=(
            jax.ShapeDtypeStruct(populations.shape, jnp.float32),
            jax.ShapeDtypeStruct(tracer.shape, jnp.float32),
        ),
        in_specs=[near],
        out_specs=(far, far),
        scratch_shapes=[
            pltpu.VMEM(populations.shape, jnp.float32),
            pltpu.VMEM(tracer.shape, jnp.float32),
            pltpu.SemaphoreType.DMA((POPS,)),
        ],
        compiler_params=pltpu.CompilerParams(vmem_limit_bytes=16 << 20),
        name="finish",
    )(pltpu.with_memory_space_constraint(relaxed, pltpu.VMEM))


def solution(mesh):
    sizes = (mesh.shape["gx"], mesh.shape["gy"])
    in_specs = (
        P(None, "gx", "gy"),
        P(None, "gx", "gy"),
        P("gx", "gy"),
        P("gx", "gy"),
        P(),
        P("gx", "gy"),
    )
    out_specs = (P(None, "gx", "gy"), P(None, "gx", "gy"))
    return jax.shard_map(
        functools.partial(local, sizes),
        mesh=mesh,
        in_specs=in_specs,
        out_specs=out_specs,
        check_vma=False,
    )
```

time: 51 us -> 40.9 us (0.80)
  Pallas kernels: 47.4 us -> 40.1 us
  local copies, waits for them, and re-layouts: 2.69 us -> 0 us
    pallas_call x1 -> x2, Pallas kernels: 47.4 us -> 40.1 us  [the longest x1 38.8 us: local(): pl.pallas_call(functools.partial(exchange, sizes), out_shape=pltpu.VMEM((...]
    unnamed x4 -> x0, local copies, waits for them, and re-layouts: 2.69 us -> none
where the time goes in v3:
time: 40.9 us; the launch traced here: 40.7 us
  Pallas kernels  40.1 us (98%)
  between operations  0.64 us (2%)
    pallas_call x1, Pallas kernels, local(): pl.pallas_call(functools.partial(exchange, sizes), out_shape=pltpu.VMEM((...  38.8 us
    pallas_call x1, Pallas kernels, local(): pl.pallas_call(finish, out_shape=(jax.ShapeDtypeStruct(populations.shape,...  1.21 us

profile of v3, /device:TPU:1, one launch (start us, length us, event | category | flops | bytes accessed | tf_op | source)
XLA Modules:
  0.0 40.7 jit_solution(4077002528072663633)
XLA Ops:
  0.6 38.8 %exchange.1.relaxed = f32[29,24,640]{2,1,0:T(8,128)S(1)} custom-call(f32[19,16,512]{2,1,0:T(8,128)} %flow_in.1, f32[7,16,512]{2,1,0:T(8,128)} %trace_in.1, s32[16,512]{1,0:T(8,128)} %solid_in.1, s32[16,512]{1,0:T(8,128)} %inflow_in.1, f32[3,32]{1,0:T(4,128)} %wind_in.1, f32[16,512]{1,0:T(8,128)} %emission_in.1), custom_call_target="tpu_custom_call" | custom-call | tf_op jit(solution)/shard_map/exchange/pallas_call | solution.py:453
  39.5 1.2 %finish.1 = (f32[19,16,512]{2,1,0:T(8,128)}, f32[7,16,512]{2,1,0:T(8,128)}) custom-call(f32[29,24,640]{2,1,0:T(8,128)S(1)} %exchange.1.relaxed), custom_call_target="tpu_custom_call" | custom-call | tf_op jit(solution)/shard_map/finish/pallas_call | solution.py:475

commit v4 on v3

--- a/solution.py
+++ b/solution.py
@@ -48,6 +48,8 @@
 SENDS = ((1, 0), (-1, 0), (0, 1), (0, -1), (1, 1), (-1, -1), (1, -1), (-1, 1))
 MESH = pl.DeviceIdType.MESH
 GROUPS = 128 // NZ
+UNROLL = 2
+UNROLL_ALL = 3
 ROW_MARGIN = 8
 LANE_MARGIN = 128
 
@@ -104,52 +106,62 @@
     total = {k: h[k] + h[k + 1] for k in range(1, FLOW, 2)}
     delta = {k: h[k] - h[k + 1] for k in range(1, FLOW, 2)}
     in_xy, in_xz, in_yz = total[7] + total[9], total[11] + total[13], total[15] + total[17]
-    along_x, along_y, along_z = 2.0 * total[1], 2.0 * total[3], 2.0 * total[5]
-    density = (
-        12.0 * h[0] + ((along_x + along_y) + along_z) + ((in_xy + in_xz) + in_yz)
-    ) * (1.0 / 36.0)
-    speed = [
-        (2.0 * delta[1] + (delta[7] + delta[9]) + (delta[11] + delta[13])) * (1.0 / 12.0),
-        (2.0 * delta[3] + (delta[7] - delta[9]) + (delta[15] + delta[17])) * (1.0 / 12.0),
-        (2.0 * delta[5] + (delta[11] - delta[13]) + (delta[15] - delta[17])) * (1.0 / 12.0),
+    twice = [total[k] + total[k] for k in (1, 3, 5)]
+    moment = [twice[0] + (in_xy + in_xz), twice[1] + (in_xy + in_yz), twice[2] + (in_xz + in_yz)]
+    density = (12.0 * h[0] + moment[0]) + ((twice[1] + twice[2]) + in_yz)
+    drive = [
+        (delta[1] + delta[1]) + ((delta[7] + delta[9]) + (delta[11] + delta[13])),
+        (delta[3] + delta[3]) + ((delta[7] - delta[9]) + (delta[15] + delta[17])),
+        (delta[5] + delta[5]) + ((delta[11] - delta[13]) + (delta[15] - delta[17])),
     ]
+    speed = [d * (1.0 / 6.0) for d in drive]
     square = [v * v for v in speed]
-    third = 3.0 * density
-    stress_x = 0.25 * (along_x + in_xy + in_xz) - third - square[0]
-    stress_y = 0.25 * (along_y + in_xy + in_yz) - third - square[1]
-    stress_z = 0.25 * (along_z + in_xz + in_yz) - third - square[2]
-    stress_xy = 0.25 * (total[7] - total[9]) - speed[0] * speed[1]
-    stress_xz = 0.25 * (total[11] - total[13]) - speed[0] * speed[2]
-    stress_yz = 0.25 * (total[15] - total[17]) - speed[1] * speed[2]
-    contraction = (
-        stress_x * stress_x
-        + stress_y * stress_y
-        + stress_z * stress_z
-        + 2.0 * (stress_xy * stress_xy + stress_xz * stress_xz + stress_yz * stress_yz)
+    cross = [speed[0] * speed[1], speed[0] * speed[2], speed[1] * speed[2]]
+    third = density * (1.0 / 3.0)
+    stress = [(moment[a] - third) - square[a] for a in range(3)]
+    shear = [
+        (total[7] - total[9]) - cross[0],
+        (total[11] - total[13]) - cross[1],
+        (total[15] - total[17]) - cross[2],
+    ]
+    sheared = (shear[0] * shear[0] + shear[1] * shear[1]) + shear[2] * shear[2]
+    contraction = ((stress[0] * stress[0] + stress[1] * stress[1]) + stress[2] * stress[2]) + (
+        sheared + sheared
     )
-    gain = 18.0 * math.sqrt(2.0) * SMAGORINSKY * SMAGORINSKY / 9.0
-    rate = 2.0 / (
-        BASE_RELAX + jnp.sqrt(BASE_RELAX * BASE_RELAX + gain * jnp.sqrt(contraction))
+    gain = 18.0 * math.sqrt(2.0) * SMAGORINSKY * SMAGORINSKY / 36.0
+    inner = BASE_RELAX * BASE_RELAX + gain * jnp.sqrt(contraction)
+    half = 1.0 / (BASE_RELAX + inner * lax.rsqrt(inner))
+    keep = 1.0 - (half + half)
+    base = half * (
+        density * (1.0 / 18.0) - ((square[0] + square[1]) + square[2]) * (1.0 / 12.0)
     )
-    keep = 1.0 - rate
-    base = rate * (density - (square[0] + square[1] + square[2]) * (1.0 / 6.0))
-    half = 0.5 * rate
+    lean = [half * v for v in speed]
+    quarter = 0.25 * half
+    bend = [quarter * v for v in square]
+    twist = [(0.5 * half) * v for v in cross]
+    straight = [base + v for v in bend]
+    slant = [straight[0] + bend[1], straight[0] + bend[2], straight[1] + bend[2]]
 
     def settle(k, fluid):
         return jnp.where(solid, h[OPPOSITE[k]], jnp.where(inflow, held(k), fluid))
 
     relaxed = [settle(0, keep * h[0] + base)]
-    for k in range(1, FLOW, 2):
-        along = sum(LATTICE[k][a] * speed[a] for a in range(3) if LATTICE[k][a] != 0)
-        even = base + half * along * along
-        odd = rate * along
+
+    def pair(k, even, odd):
         relaxed.append(settle(k, keep * h[k] + (even + odd)))
         relaxed.append(settle(k + 1, keep * h[k + 1] + (even - odd)))
 
-    amount = 0.25 * q[0] + 0.125 * ((q[1] + q[2]) + (q[3] + q[4]) + (q[5] + q[6]))
-    share = amount * (1.0 / TRACER_RELAX)
+    for a in range(3):
+        pair(2 * a + 1, straight[a], lean[a])
+    for i, (a, b) in enumerate(((0, 1), (0, 2), (1, 2))):
+        pair(4 * i + 7, slant[i] + twist[i], lean[a] + lean[b])
+        pair(4 * i + 9, slant[i] - twist[i], lean[a] - lean[b])
+
+    share = (0.25 / TRACER_RELAX) * q[0] + (0.125 / TRACER_RELAX) * (
+        (q[1] + q[2]) + (q[3] + q[4]) + (q[5] + q[6])
+    )
     level = share + emission
-    drift = share * (4.0 / 3.0)
+    drift = share * (2.0 / 3.0)
     rest = 1.0 - 1.0 / TRACER_RELAX
 
     def trace(k, fluid):
@@ -157,9 +169,9 @@
 
     traced = [trace(0, rest * q[0] + level)]
     for k in range(1, TRACE, 2):
-        lean = drift * speed[(k - 1) // 2]
-        traced.append(trace(k, rest * q[k] + (level + lean)))
-        traced.append(trace(k + 1, rest * q[k + 1] + (level - lean)))
+        carried = drift * speed[(k - 1) // 2]
+        traced.append(trace(k, rest * q[k] + (level + carried)))
+        traced.append(trace(k + 1, rest * q[k + 1] + (level - carried)))
     return relaxed, traced
 
 
@@ -223,23 +235,36 @@
     relaxed[POPS, pl.ds(0, rows), pl.ds(0, width)] = jnp.where(solid[...] == 1, 1.0, 0.0)
     relaxed[POPS + 1, pl.ds(0, rows), pl.ds(0, width)] = jnp.where(inflow[...] == 1, 1.0, 0.0)
 
-    def relax(row_tiles, lane_tiles):
-        def tile(index, carry):
-            row = pl.ds(pl.multiple_of((index // lane_tiles) * 8, 8), 8)
-            lane = pl.ds(pl.multiple_of((index % lane_tiles) * 128, 128), 128)
-            settled, traced = relax_cells(
-                [state[k, row, lane] for k in range(FLOW)],
-                [state[FLOW + k, row, lane] for k in range(TRACE)],
-                relaxed[POPS, row, lane] == 1.0,
-                relaxed[POPS + 1, row, lane] == 1.0,
-                relaxed[POPS + 2, row, lane],
-                lambda k: held[k],
-            )
-            for k, cells in enumerate(settled + traced):
-                relaxed[k, row, lane] = cells
+    def relax_tile(row_tile, lane_tile):
+        row = pl.ds(pl.multiple_of(row_tile * 8, 8), 8)
+        lane = pl.ds(pl.multiple_of(lane_tile * 128, 128), 128)
+        settled, traced = relax_cells(
+            [state[k, row, lane] for k in range(FLOW)],
+            [state[FLOW + k, row, lane] for k in range(TRACE)],
+            relaxed[POPS, row, lane] == 1.0,
+            relaxed[POPS + 1, row, lane] == 1.0,
+            relaxed[POPS + 2, row, lane],
+            lambda k: held[k],
+        )
+        for k, cells in enumerate(settled + traced):
+            relaxed[k, row, lane] = cells
+
+    def relax(row_tiles, lane_tiles, unroll):
+        def tiles(index, carry):
+            for i in range(unroll):
+                at = index * unroll + i
+                relax_tile(at // lane_tiles, at % lane_tiles)
             return carry
 
-        lax.fori_loop(0, row_tiles * lane_tiles, tile, 0)
+        lax.fori_loop(0, row_tiles * lane_tiles // unroll, tiles, 0)
+
+    def relax_row(row_tile, unroll):
+        def tiles(index, carry):
+            for i in range(unroll):
+                relax_tile(row_tile, index * unroll + i)
+            return carry
+
+        lax.fori_loop(0, chunks // unroll, tiles, 0)
 
     group = lax.broadcasted_iota(jnp.int32, (8, 128), 1) // NZ
 
@@ -271,14 +296,14 @@
                 count = min(8, height - top)
                 box[i, pl.ds(top, count), :] = merge(pieces)[:count]
 
-    def pack_rows(planes, box):
-        for i, sign in enumerate((1, -1)):
-            for u, (k, n) in enumerate(row_units(planes, sign)):
-                row = rows - 1 - n if sign > 0 else n
-                for c in range(chunks):
-                    box[i, pl.ds(u * chunks + c, 1), :] = relaxed[
-                        k, pl.ds(row, 1), pl.ds(c * 128, 128)
-                    ]
+    def pack_rows(planes, box, i):
+        sign = SENDS[i][0]
+        for u, (k, n) in enumerate(row_units(planes, sign)):
+            row = rows - 1 - n if sign > 0 else n
+            for c in range(chunks):
+                box[i, pl.ds(u * chunks + c, 1), :] = relaxed[
+                    k, pl.ds(row, 1), pl.ds(c * 128, 128)
+                ]
 
     def pack_columns(planes, box):
         for i, sign in enumerate((1, -1)):
@@ -342,6 +367,41 @@
                     )
 
     height = lax.broadcasted_iota(jnp.int32, (tall, wide), 1) % NZ
+
+    near = lax.broadcasted_iota(jnp.int32, (8, wide), 1) % NZ
+    edge = lax.broadcasted_iota(jnp.int32, (8, wide), 0)
+
+    def pass_margin():
+        last = pl.ds(rows - 8, 8)
+        outer = pl.ds(rows, 8)
+        first = pl.ds(0, 8)
+        for k in range(POPS):
+            step_x, step_y, step_z = MOVES[k]
+            by = (step_y * NZ + step_z) % wide
+
+            def along(at, k=k, by=by):
+                return pltpu.roll(relaxed[k, at, :], by, 1) if by else relaxed[k, at, :]
+
+            cells = along(outer)
+            if step_x > 0:
+                turn = pltpu.roll(cells, 1, 0)
+                cells = jnp.where(edge == 0, pltpu.roll(along(last), 1, 0), turn)
+                take = edge == 0
+                if step_z:
+                    take = take & (near != (0 if step_z == 1 else NZ - 1))
+                state[k, first, :] = jnp.where(take, turn, state[k, first, :])
+            elif step_x < 0:
+                turn = pltpu.roll(cells, 7, 0)
+                cells = jnp.where(edge == 7, pltpu.roll(along(first), 7, 0), turn)
+                take = edge == 7
+                if step_z:
+                    take = take & (near != (0 if step_z == 1 else NZ - 1))
+                state[k, last, :] = jnp.where(take, turn, state[k, last, :])
+            if step_z:
+                cells = jnp.where(
+                    near == (0 if step_z == 1 else NZ - 1), relaxed[BACK[k], outer, :], cells
+                )
+            state[k, outer, :] = cells
 
     def copies(step):
         x_out, x_got, y_out, y_got, c_out, c_got = boxes[6 * step : 6 * step + 6]
@@ -369,21 +429,39 @@
         planes = POPS if step else PLANES
         x_out, x_got, y_out, y_got, c_out, c_got = boxes[6 * step : 6 * step + 6]
         sent = copies(step)
-        relax(rows // 8, chunks)
-        pack_rows(planes, x_out)
+        upper = lax.rem(gx, 2)
+        last = rows // 8 - 1
+        relax_row(upper * last, UNROLL)
+        for index in range(1, last):
+            relax_row(index, UNROLL)
         if step == 0:
             pl.semaphore_wait(barrier, 8)
         for side in (0, 1):
+
+            @pl.when(upper == 1 - side)
+            def _():
+                pack_rows(planes, x_out, side)
+                sent[side].start()
+
+        relax_row((1 - upper) * last, UNROLL)
+        pack_columns(planes, y_out)
+        for side in (2, 3):
             sent[side].start()
         pack_corners(planes, c_out)
         for side in range(4, 8):
             sent[side].start()
-        pack_columns(planes, y_out)
-        for side in (2, 3):
-            sent[side].start()
+        for side in (0, 1):
+
+            @pl.when(upper == side)
+            def _():
+                pack_rows(planes, x_out, side)
+                sent[side].start()
+
         for side in (2, 3):
             sent[side].wait_recv()
         unpack_columns(planes, y_got)
+        for k in range(POPS):
+            state[k, pl.ds(0, rows), :] = passed(relaxed, k, height)[:rows]
         for side in (4, 5, 6, 7):
             sent[side].wait_recv()
         unpack_corners(planes, c_got)
@@ -392,9 +470,8 @@
         unpack_rows(planes, x_got)
         for copy in sent:
             copy.wait_send()
-        for k in range(POPS):
-            state[k] = passed(relaxed, k, height)
-        relax(tall // 8, wide // 128)
+        pass_margin()
+        relax(tall // 8, wide // 128, UNROLL_ALL)
         if step < ROUNDS - 1:
             for k in range(POPS):
                 state[k, pl.ds(0, rows), pl.ds(0, width)] = passed(relaxed, k, height)[

time: 40.9 us -> 40.5 us (level)
  no operation moved by 1% of the time
where the time goes in v4:
time: 40.5 us; the launch traced here: 40.3 us
  Pallas kernels  39.7 us (98%)
  between operations  0.64 us (2%)
    pallas_call x1, Pallas kernels, local(): pl.pallas_call(functools.partial(exchange, sizes), out_shape=pltpu.VMEM((...  38.5 us
    pallas_call x1, Pallas kernels, local(): pl.pallas_call(finish, out_shape=(jax.ShapeDtypeStruct(populations.shape,...  1.21 us

profile of v4, /device:TPU:1, one launch (start us, length us, event | category | flops | bytes accessed | tf_op | source)
XLA Modules:
  0.0 40.3 jit_solution(15606077148123145563)
XLA Ops:
  0.6 38.5 %exchange.1.relaxed = f32[29,24,640]{2,1,0:T(8,128)S(1)} custom-call(f32[19,16,512]{2,1,0:T(8,128)} %flow_in.1, f32[7,16,512]{2,1,0:T(8,128)} %trace_in.1, s32[16,512]{1,0:T(8,128)} %solid_in.1, s32[16,512]{1,0:T(8,128)} %inflow_in.1, f32[3,32]{1,0:T(4,128)} %wind_in.1, f32[16,512]{1,0:T(8,128)} %emission_in.1), custom_call_target="tpu_custom_call" | custom-call | tf_op jit(solution)/shard_map/exchange/pallas_call | solution.py:530
  39.1 1.2 %finish.1 = (f32[19,16,512]{2,1,0:T(8,128)}, f32[7,16,512]{2,1,0:T(8,128)}) custom-call(f32[29,24,640]{2,1,0:T(8,128)S(1)} %exchange.1.relaxed), custom_call_target="tpu_custom_call" | custom-call | tf_op jit(solution)/shard_map/finish/pallas_call | solution.py:552

commit v5 on v4

--- a/solution.py
+++ b/solution.py
@@ -193,6 +193,8 @@
     in_sem,
     send_sem,
     recv_sem,
+    passing,
+    pass_sem,
     *boxes,
 ):
     rows, width = solid.shape
@@ -207,9 +209,29 @@
             lax.rem(gy + step_y + sizes[1], sizes[1]),
         )
 
+    upper = lax.rem(gx, 2)
+    plane = lax.rem(gx // 2, 2) * 4 + lax.rem(gy, 4)
+    first_out = [
+        jnp.logical_not((plane == 0) & (upper == {6: 1, 5: 0}[side]))
+        if side in (5, 6)
+        else None
+        for side in range(8)
+    ]
+
     barrier = pltpu.get_barrier_semaphore()
+
+    def greet(side):
+        pl.semaphore_signal(barrier, inc=1, device_id=device(side), device_id_type=MESH)
+
     for side in range(8):
-        pl.semaphore_signal(barrier, inc=1, device_id=device(side), device_id_type=MESH)
+        if side in (4, 7):
+
+            @pl.when(jnp.logical_not((plane == 7) & (upper == {4: 1, 7: 0}[side])))
+            def _():
+                greet(side)
+
+        else:
+            greet(side)
 
     block = (slice(None), pl.ds(0, rows), pl.ds(0, width))
     loads = [
@@ -279,22 +301,27 @@
         by = by * NZ % 128
         return pltpu.roll(piece, by, 1) if by else piece
 
+    def pack_corner(planes, box, i, side, row_of):
+        sign_x, sign_y = SENDS[side]
+        lane = width - 128 if sign_y > 0 else 0
+        height, places = corner_units(planes, sign_x, sign_y)
+        for j, units in enumerate(places):
+            for u, (k, n, m) in enumerate(units):
+                stage[i, j, pl.ds(u, 1), :] = relaxed[k, pl.ds(row_of(n), 1), pl.ds(lane, 128)]
+        for top in range(0, height, 8):
+            pieces = []
+            for j in range(4):
+                m = 1 if j == 3 else 0
+                own = GROUPS - 1 - m if sign_y > 0 else m
+                pieces.append((turned(stage[i, j, pl.ds(top, 8), :], j - own), [j]))
+            count = min(8, height - top)
+            box[i, pl.ds(top, count), :] = merge(pieces)[:count]
+
     def pack_corners(planes, box):
-        for i, (sign_x, sign_y) in enumerate(SENDS[4:]):
-            lane = width - 128 if sign_y > 0 else 0
-            height, places = corner_units(planes, sign_x, sign_y)
-            for j, units in enumerate(places):
-                for u, (k, n, m) in enumerate(units):
-                    row = rows - 1 - n if sign_x > 0 else n
-                    stage[i, j, pl.ds(u, 1), :] = relaxed[k, pl.ds(row, 1), pl.ds(lane, 128)]
-            for top in range(0, height, 8):
-                pieces = []
-                for j in range(4):
-                    m = 1 if j == 3 else 0
-                    own = GROUPS - 1 - m if sign_y > 0 else m
-                    pieces.append((turned(stage[i, j, pl.ds(top, 8), :], j - own), [j]))
-                count = min(8, height - top)
-                box[i, pl.ds(top, count), :] = merge(pieces)[:count]
+        for i, (sign_x, _) in enumerate(SENDS[4:]):
+            pack_corner(
+                planes, box, i, 4 + i, (lambda n: rows - 1 - n) if sign_x > 0 else (lambda n: n)
+            )
 
     def pack_rows(planes, box, i):
         sign = SENDS[i][0]
@@ -322,14 +349,14 @@
                         ]
                     )
 
-    def unpack_rows(planes, box):
-        for i, sign in enumerate((1, -1)):
-            for u, (k, n) in enumerate(row_units(planes, sign)):
-                row = tall - 1 - n if sign > 0 else rows + n
-                for c in range(chunks):
-                    relaxed[k, pl.ds(row, 1), pl.ds(c * 128, 128)] = box[
-                        i, pl.ds(u * chunks + c, 1), :
-                    ]
+    def unpack_rows(planes, box, i):
+        sign = SENDS[i][0]
+        for u, (k, n) in enumerate(row_units(planes, sign)):
+            row = tall - 1 - n if sign > 0 else rows + n
+            for c in range(chunks):
+                relaxed[k, pl.ds(row, 1), pl.ds(c * 128, 128)] = box[
+                    i, pl.ds(u * chunks + c, 1), :
+                ]
 
     def unpack_columns(planes, box):
         for top in range(0, rows, 8):
@@ -402,6 +429,16 @@
                     near == (0 if step_z == 1 else NZ - 1), relaxed[BACK[k], outer, :], cells
                 )
             state[k, outer, :] = cells
+
+    def carry_on(side):
+        return pltpu.make_async_remote_copy(
+            src_ref=passing.at[0],
+            dst_ref=boxes[5].at[side - 4],
+            send_sem=pass_sem,
+            recv_sem=recv_sem.at[0, side],
+            device_id=device(3),
+            device_id_type=MESH,
+        )
 
     def copies(step):
         x_out, x_got, y_out, y_got, c_out, c_got = boxes[6 * step : 6 * step + 6]
@@ -429,13 +466,12 @@
         planes = POPS if step else PLANES
         x_out, x_got, y_out, y_got, c_out, c_got = boxes[6 * step : 6 * step + 6]
         sent = copies(step)
-        upper = lax.rem(gx, 2)
         last = rows // 8 - 1
         relax_row(upper * last, UNROLL)
         for index in range(1, last):
             relax_row(index, UNROLL)
         if step == 0:
-            pl.semaphore_wait(barrier, 8)
+            pl.semaphore_wait(barrier, jnp.where(plane == 0, 7, 8))
         for side in (0, 1):
 
             @pl.when(upper == 1 - side)
@@ -449,13 +485,33 @@
             sent[side].start()
         pack_corners(planes, c_out)
         for side in range(4, 8):
-            sent[side].start()
+            if step == 0 and first_out[side] is not None:
+                pl.when(first_out[side])(sent[side].start)
+            else:
+                sent[side].start()
         for side in (0, 1):
 
             @pl.when(upper == side)
             def _():
                 pack_rows(planes, x_out, side)
                 sent[side].start()
+
+        if step == 0:
+            for side in (0, 1):
+
+                @pl.when((plane == 4) & (upper == side))
+                def _():
+                    sent[side].wait_recv()
+                    unpack_rows(planes, x_got, side)
+                    onward = 6 - side
+                    pack_corner(
+                        planes,
+                        passing,
+                        0,
+                        onward,
+                        (lambda n: tall - 1 - n) if side == 0 else (lambda n: rows + n),
+                    )
+                    carry_on(onward).start()
 
         for side in (2, 3):
             sent[side].wait_recv()
@@ -466,10 +522,27 @@
             sent[side].wait_recv()
         unpack_corners(planes, c_got)
         for side in (0, 1):
-            sent[side].wait_recv()
-        unpack_rows(planes, x_got)
-        for copy in sent:
-            copy.wait_send()
+
+            def take_rows(side=side):
+                sent[side].wait_recv()
+                unpack_rows(planes, x_got, side)
+
+            if step == 0:
+                pl.when(jnp.logical_not((plane == 4) & (upper == side)))(take_rows)
+            else:
+                take_rows()
+        for side in range(8):
+            if step == 0 and first_out[side] is not None:
+                pl.when(first_out[side])(sent[side].wait_send)
+            else:
+                sent[side].wait_send()
+        if step == 0:
+            for side in (0, 1):
+
+                @pl.when((plane == 4) & (upper == side))
+                def _():
+                    carry_on(6 - side).wait_send()
+
         pass_margin()
         relax(tall // 8, wide // 128, UNROLL_ALL)
         if step < ROUNDS - 1:
@@ -542,6 +615,8 @@
             pltpu.SemaphoreType.DMA((6,)),
             pltpu.SemaphoreType.DMA((ROUNDS, 8)),
             pltpu.SemaphoreType.DMA((ROUNDS, 8)),
+            pltpu.VMEM((1, CORNER_OF[0], 128), jnp.float32),
+            pltpu.SemaphoreType.DMA,
             *boxes,
         ],
         compiler_params=pltpu.CompilerParams(

time: 40.5 us -> 40.2 us (level)
  no operation moved by 1% of the time
where the time goes in v5:
time: 40.2 us; the launch traced here: 40.1 us
  Pallas kernels  39.4 us (98%)
  between operations  0.64 us (2%)
    pallas_call x1, Pallas kernels, local(): pl.pallas_call(functools.partial(exchange, sizes), out_shape=pltpu.VMEM((...  38.2 us
    pallas_call x1, Pallas kernels, local(): pl.pallas_call(finish, out_shape=(jax.ShapeDtypeStruct(populations.shape,...  1.21 us

profile of v5, /device:TPU:1, one launch (start us, length us, event | category | flops | bytes accessed | tf_op | source)
XLA Modules:
  0.0 40.1 jit_solution(17856648971135778021)
XLA Ops:
  0.6 38.2 %exchange.1.relaxed = f32[29,24,640]{2,1,0:T(8,128)S(1)} custom-call(f32[19,16,512]{2,1,0:T(8,128)} %flow_in.1, f32[7,16,512]{2,1,0:T(8,128)} %trace_in.1, s32[16,512]{1,0:T(8,128)} %solid_in.1, s32[16,512]{1,0:T(8,128)} %inflow_in.1, f32[3,32]{1,0:T(4,128)} %wind_in.1, f32[16,512]{1,0:T(8,128)} %emission_in.1), custom_call_target="tpu_custom_call" | custom-call | tf_op jit(solution)/shard_map/exchange/pallas_call | solution.py:603
  38.9 1.2 %finish.1 = (f32[19,16,512]{2,1,0:T(8,128)}, f32[7,16,512]{2,1,0:T(8,128)}) custom-call(f32[29,24,640]{2,1,0:T(8,128)S(1)} %exchange.1.relaxed), custom_call_target="tpu_custom_call" | custom-call | tf_op jit(solution)/shard_map/finish/pallas_call | solution.py:627

commit v6 on v5

--- a/solution.py
+++ b/solution.py
@@ -471,30 +471,44 @@
         for index in range(1, last):
             relax_row(index, UNROLL)
         if step == 0:
+            relax_row((1 - upper) * last, UNROLL)
+            for side in (0, 1):
+                pack_rows(planes, x_out, side)
+            pack_columns(planes, y_out)
+            pack_corners(planes, c_out)
             pl.semaphore_wait(barrier, jnp.where(plane == 0, 7, 8))
-        for side in (0, 1):
-
-            @pl.when(upper == 1 - side)
-            def _():
-                pack_rows(planes, x_out, side)
+            for side in (0, 1):
+                pl.when(upper == 1 - side)(sent[side].start)
+            for side in (2, 3):
                 sent[side].start()
-
-        relax_row((1 - upper) * last, UNROLL)
-        pack_columns(planes, y_out)
-        for side in (2, 3):
-            sent[side].start()
-        pack_corners(planes, c_out)
-        for side in range(4, 8):
-            if step == 0 and first_out[side] is not None:
-                pl.when(first_out[side])(sent[side].start)
-            else:
+            for side in range(4, 8):
+                if first_out[side] is not None:
+                    pl.when(first_out[side])(sent[side].start)
+                else:
+                    sent[side].start()
+            for side in (0, 1):
+                pl.when(upper == side)(sent[side].start)
+        else:
+            for side in (0, 1):
+
+                @pl.when(upper == 1 - side)
+                def _():
+                    pack_rows(planes, x_out, side)
+                    sent[side].start()
+
+            relax_row((1 - upper) * last, UNROLL)
+            pack_columns(planes, y_out)
+            for side in (2, 3):
                 sent[side].start()
-        for side in (0, 1):
-
-            @pl.when(upper == side)
-            def _():
-                pack_rows(planes, x_out, side)
+            pack_corners(planes, c_out)
+            for side in range(4, 8):
                 sent[side].start()
+            for side in (0, 1):
+
+                @pl.when(upper == side)
+                def _():
+                    pack_rows(planes, x_out, side)
+                    sent[side].start()
 
         if step == 0:
             for side in (0, 1):
@@ -531,18 +545,6 @@
                 pl.when(jnp.logical_not((plane == 4) & (upper == side)))(take_rows)
             else:
                 take_rows()
-        for side in range(8):
-            if step == 0 and first_out[side] is not None:
-                pl.when(first_out[side])(sent[side].wait_send)
-            else:
-                sent[side].wait_send()
-        if step == 0:
-            for side in (0, 1):
-
-                @pl.when((plane == 4) & (upper == side))
-                def _():
-                    carry_on(6 - side).wait_send()
-
         pass_margin()
         relax(tall // 8, wide // 128, UNROLL_ALL)
         if step < ROUNDS - 1:
@@ -550,6 +552,15 @@
                 state[k, pl.ds(0, rows), pl.ds(0, width)] = passed(relaxed, k, height)[
                     :rows, :width
                 ]
+
+    for step in range(ROUNDS):
+        for side, copy in enumerate(copies(step)):
+            if step == 0 and first_out[side] is not None:
+                pl.when(first_out[side])(copy.wait_send)
+            else:
+                copy.wait_send()
+    for side in (0, 1):
+        pl.when((plane == 4) & (upper == side))(carry_on(6 - side).wait_send)
 
 
 def passed(relaxed, k, height):

time: 40.2 us -> 39.9 us (level)
  no operation moved by 1% of the time
where the time goes in v6:
time: 39.9 us; the launch traced here: 39.7 us
  Pallas kernels  39.1 us (98%)
  between operations  0.64 us (2%)
    pallas_call x1, Pallas kernels, local(): pl.pallas_call(functools.partial(exchange, sizes), out_shape=pltpu.VMEM((...  37.9 us
    pallas_call x1, Pallas kernels, local(): pl.pallas_call(finish, out_shape=(jax.ShapeDtypeStruct(populations.shape,...  1.21 us

profile of v6, /device:TPU:1, one launch (start us, length us, event | category | flops | bytes accessed | tf_op | source)
XLA Modules:
  0.0 39.7 jit_solution(15015653205944549634)
XLA Ops:
  0.6 37.9 %exchange.1.relaxed = f32[29,24,640]{2,1,0:T(8,128)S(1)} custom-call(f32[19,16,512]{2,1,0:T(8,128)} %flow_in.1, f32[7,16,512]{2,1,0:T(8,128)} %trace_in.1, s32[16,512]{1,0:T(8,128)} %solid_in.1, s32[16,512]{1,0:T(8,128)} %inflow_in.1, f32[3,32]{1,0:T(4,128)} %wind_in.1, f32[16,512]{1,0:T(8,128)} %emission_in.1), custom_call_target="tpu_custom_call" | custom-call | tf_op jit(solution)/shard_map/exchange/pallas_call | solution.py:614
  38.5 1.2 %finish.1 = (f32[19,16,512]{2,1,0:T(8,128)}, f32[7,16,512]{2,1,0:T(8,128)}) custom-call(f32[29,24,640]{2,1,0:T(8,128)S(1)} %exchange.1.relaxed), custom_call_target="tpu_custom_call" | custom-call | tf_op jit(solution)/shard_map/finish/pallas_call | solution.py:638
